TPU v7x, 8 devices: a whole 2x2x1 slice. The times are simulated.
8 devices in a mesh: q: 8 (over z, y, x, core).
Axes of the slice: x: 2, y: 2, z: 1, core: 2. Of those that a mesh axis runs over, the one named last changes fastest.
Arguments:
- state_in: float32 [2, 1048576], P(None, 'q')
- unitaries: float32 [2, 20, 2, 2], replicated
- cz_pairs: int32 [10, 2], replicated
Outputs:
- output 1: float32 [2, 1048576], P(None, 'q')
- output 2: float32 [20], replicated
All inputs are finite; a program needn't handle non-finite values.
Results may differ from a plain program's by a relative error of at most 0.001.
Values sent between devices are 32-bit elements.
A program may use at most 1 GiB of HBM per device.

v0:
```python
import jax
import jax.numpy as jnp
from jax import lax
from jax.sharding import PartitionSpec as P

LOW_BITS = 7
LANES = 2 ** LOW_BITS


def mix_pair(first, second, coef_a, coef_b):
    out_re = coef_a[0] * first[0] - coef_a[1] * first[1] + coef_b[0] * second[0] - coef_b[1] * second[1]
    out_im = coef_a[0] * first[1] + coef_a[1] * first[0] + coef_b[0] * second[1] + coef_b[1] * second[0]
    return jnp.stack([out_re, out_im])


def gate_wide(state, bit_pos, gate_mat):
    stride = state.shape[1] >> (bit_pos + 1)
    if stride >= 8 * LANES:
        view = state.reshape(2, 2 ** bit_pos, 2, stride // LANES, LANES)
        zero_half = view[:, :, 0]
        one_half = view[:, :, 1]
        new_zero = mix_pair(zero_half, one_half, gate_mat[:, 0, 0], gate_mat[:, 0, 1])
        new_one = mix_pair(zero_half, one_half, gate_mat[:, 1, 0], gate_mat[:, 1, 1])
        return jnp.stack([new_zero, new_one], axis=2).reshape(state.shape)
    view = state.reshape(2, 2 ** bit_pos, 2 * stride)
    zero_half = view[:, :, :stride]
    one_half = view[:, :, stride:]
    new_zero = mix_pair(zero_half, one_half, gate_mat[:, 0, 0], gate_mat[:, 0, 1])
    new_one = mix_pair(zero_half, one_half, gate_mat[:, 1, 0], gate_mat[:, 1, 1])
    return jnp.concatenate([new_zero, new_one], axis=2).reshape(state.shape)


def low_block(state, low_gates):
    block_re = jnp.ones((1, 1), jnp.float32)
    block_im = jnp.zeros((1, 1), jnp.float32)
    for bit_pos in range(LOW_BITS):
        tr_re = low_gates[0, bit_pos].T
        tr_im = low_gates[1, bit_pos].T
        next_re = block_re[:, None, :, None] * tr_re[None, :, None, :] - block_im[:, None, :, None] * tr_im[None, :, None, :]
        next_im = block_re[:, None, :, None] * tr_im[None, :, None, :] + block_im[:, None, :, None] * tr_re[None, :, None, :]
        block_size = 2 * block_re.shape[0]
        block_re = next_re.reshape(block_size, block_size)
        block_im = next_im.reshape(block_size, block_size)
    rows = state.reshape(2, -1, LANES)
    highest = lax.Precision.HIGHEST
    out_re = jnp.dot(rows[0], block_re, precision=highest, preferred_element_type=jnp.float32) - jnp.dot(rows[1], block_im, precision=highest, preferred_element_type=jnp.float32)
    out_im = jnp.dot(rows[0], block_im, precision=highest, preferred_element_type=jnp.float32) + jnp.dot(rows[1], block_re, precision=highest, preferred_element_type=jnp.float32)
    return jnp.stack([out_re, out_im]).reshape(state.shape)


def sign_grid(first_index, row_count, cz_pairs, num_qubits):
    row_index = lax.iota(jnp.int32, row_count)[:, None]
    col_index = lax.iota(jnp.int32, LANES)[None, :]
    flat_index = first_index + row_index * LANES + col_index
    parity = jnp.zeros_like(flat_index)
    for pair_pos in range(cz_pairs.shape[0]):
        shift_a = num_qubits - 1 - cz_pairs[pair_pos, 0]
        shift_b = num_qubits - 1 - cz_pairs[pair_pos, 1]
        parity = parity ^ ((flat_index >> shift_a) & (flat_index >> shift_b) & 1)
    return (1 - 2 * parity).astype(jnp.float32)


def bit_balance(density, row_bits):
    row_tot = jnp.sum(density, axis=1)
    col_tot = jnp.sum(density, axis=0)
    row_index = lax.iota(jnp.int32, density.shape[0])
    col_index = lax.iota(jnp.int32, LANES)
    row_part = [jnp.sum(row_tot * (1 - 2 * ((row_index >> (row_bits - 1 - bit_pos)) & 1)).astype(jnp.float32)) for bit_pos in range(row_bits)]
    col_part = [jnp.sum(col_tot * (1 - 2 * ((col_index >> (LOW_BITS - 1 - bit_pos)) & 1)).astype(jnp.float32)) for bit_pos in range(LOW_BITS)]
    return row_part + col_part


def solution(mesh):
    group_size = mesh.shape['q']
    top_bits = group_size.bit_length() - 1

    def local_layer(state_local, unitaries, cz_pairs):
        num_qubits = unitaries.shape[1]
        local_size = state_local.shape[1]
        row_count = local_size // LANES
        device = lax.axis_index('q')
        grid = state_local.reshape(2, row_count, LANES)
        for qubit_pos in range(top_bits):
            bit_shift = top_bits - 1 - qubit_pos
            flip_mask = 1 << bit_shift
            partner = lax.ppermute(grid, 'q', [(source, source ^ flip_mask) for source in range(group_size)])
            own_bit = (device >> bit_shift) & 1
            gate_mat = unitaries[:, qubit_pos]
            coef_self = jnp.where(own_bit == 1, gate_mat[:, 1, 1], gate_mat[:, 0, 0])
            coef_other = jnp.where(own_bit == 1, gate_mat[:, 1, 0], gate_mat[:, 0, 1])
            grid = mix_pair(grid, partner, coef_self, coef_other)
        state = grid.reshape(2, local_size)
        for qubit_pos in range(top_bits, num_qubits - LOW_BITS):
            state = gate_wide(state, qubit_pos - top_bits, unitaries[:, qubit_pos])
        state = low_block(state, unitaries[:, num_qubits - LOW_BITS:])
        grid = state.reshape(2, row_count, LANES) * sign_grid(device * local_size, row_count, cz_pairs, num_qubits)[None]
        density = grid[0] * grid[0] + grid[1] * grid[1]
        local_total = jnp.sum(density)
        top_part = [jnp.where(((device >> (top_bits - 1 - qubit_pos)) & 1) == 0, local_total, -local_total) for qubit_pos in range(top_bits)]
        low_part = bit_balance(density, num_qubits - top_bits - LOW_BITS)
        z_expect = lax.psum(jnp.stack(top_part + low_part), 'q') / (local_size * group_size)
        return grid.reshape(2, local_size), z_expect

    return jax.shard_map(local_layer, mesh=mesh, in_specs=(P(None, 'q'), P(), P()), out_specs=(P(None, 'q'), P()), check_vma=False)
```

profile of v0, /device:TPU:1, one launch (start us, length us, event | category | flops | bytes accessed | tf_op | source)
XLA Modules:
  0.0 191.6 jit_solution(1485781784273932490)
XLA Ops:
  0.6 1.3 copy.195
  1.9 2.1 %collective-permute-start = (f32[2,1024,128]{2,1,0:T(8,128)S(1)}, f32[2,1024,128]{2,1,0:T(8,128)S(1)}, u32[]{:S(2)}, u32[]{:S(2)}) collective-permute-start(f32[2,1024,128]{2,1,0:T(8,128)S(1)} %bitcast.617), channel_id=1, source_target_pairs={{0,4},{1,5},{2,6},{3,7},{4,0},{5,1},{6,2},{7,3}} | collective-permute-start | bytes 3145736 | tf_op jit(solution)/shard_map/ppermute | solution.py:86
  4.0 1.4 slice_reduce_fusion.12
  5.4 1.1 slice_reduce_fusion.14
  7.2 4.1 %multiply_subtract_fusion.5 = (f32[1,131072]{1,0:T(1,128)S(1)}, f32[1,131072]{1,0:T(1,128)S(1)}) fusion(f32[2,131072]{1,0:T(2,128)} %param.3, f32[]{:T(128)} %bitcast.13, f32[]{:T(128)} %bitcast.12), kind=kLoop, calls=%fused_computation.46 | loop fusion | flops 786432 | bytes 2097160 | tf_op jit(solution)/shard_map/sub | solution.py:11
  12.9 0.8 multiply_subtract_fusion.6
  13.8 1.1 add.1079
  15.7 11.1 %collective-permute-done = f32[2,1024,128]{2,1,0:T(8,128)S(1)} collective-permute-done((f32[2,1024,128]{2,1,0:T(8,128)S(1)}, f32[2,1024,128]{2,1,0:T(8,128)S(1)}, u32[]{:S(2)}, u32[]{:S(2)}) %collective-permute-start) | collective-permute-done | bytes 1048608 | tf_op jit(solution)/shard_map/ppermute | solution.py:86
  26.9 1.4 multiply_subtract_fusion.4
  28.3 1.0 pad_maximum_fusion
  29.4 1.2 collective-permute-start.1
  32.4 3.9 %multiply_subtract_fusion = (f32[64,2,64,2]{3,2,1,0:T(8,128)}, f32[64,2,64,2]{3,2,1,0:T(8,128)}) fusion(f32[2,2]{1,0:T(2,128)S(1)} %copy.177, f32[64,64]{1,0:T(8,128)S(1)} %add.1081, f32[2,2]{1,0:T(2,128)S(1)} %copy.176, f32[64,64]{1,0:T(8,128)S(1)} %sub.767), kind=kLoop, calls=%fused_computation.1 | loop fusion | flops 98304 | bytes 163872 | tf_op jit(solution)/shard_map/sub | solution.py:39
  36.3 4.0 %sub.769 = f32[128,128]{1,0:T(8,128)S(1)} reshape(f32[64,2,64,2]{3,2,1,0:T(8,128)} %get-tuple-element.89) | data formatting | bytes 131072 | tf_op jit(solution)/shard_map/sub | solution.py:39
  40.3 4.2 %add.1083 = f32[128,128]{1,0:T(8,128)S(1)} reshape(f32[64,2,64,2]{3,2,1,0:T(8,128)} %get-tuple-element.90) | data formatting | bytes 131072 | tf_op jit(solution)/shard_map/add | solution.py:40
  59.7 4.0 %multiply_add_fusion.3 = (f32[1,1024,128]{2,1,0:T(8,128)S(1)}, f32[1,1024,128]{2,1,0:T(8,128)S(1)}) fusion(f32[1,1024,128]{2,1,0:T(8,128)S(1)} %get-tuple-element.85, f32[1,1024,128]{2,1,0:T(8,128)S(1)} %get-tuple-element.86, f32[2,1024,128]{2,1,0:T(8,128)} %collective-permute-done.1, f32[]{:T(128)} %bitcast.20, f32[]{:T(128)} %bitcast.19, f32[]{:T(128)} %bitcast.17, ...), kind=kLoop, calls=%fused_computation.41 | loop fusion | flops 1835008 | bytes 3145744 | tf_op jit(solution)/shard_map/add | solution.py:12
  63.8 1.8 collective-permute-start.2
  69.7 1.0 subtract_convert_fusion
  70.7 2.9 %multiply_subtract_fusion.2 = (f32[1,1024,128]{2,1,0:T(8,128)S(1)}, f32[1,1024,128]{2,1,0:T(8,128)S(1)}) fusion(f32[1,1024,128]{2,1,0:T(8,128)S(1)} %get-tuple-element.51, f32[1,1024,128]{2,1,0:T(8,128)S(1)} %get-tuple-element.52, f32[2,1024,128]{2,1,0:T(8,128)S(1)} %collective-permute-done.2, f32[]{:T(128)} %bitcast.23, f32[]{:T(128)} %bitcast.22, ...), kind=kLoop, calls=%fused_computation.40 | loop fusion | flops 1835008 | bytes 3145744 | tf_op jit(solution)/shard_map/sub | solution.py:11
  73.6 5.1 %multiply_subtract_fusion.14 = (f32[1,1,1,512,128]{4,3,2,1,0:T(8,128)S(1)}, f32[1,1,1,512,128]{4,3,2,1,0:T(8,128)S(1)}) fusion(f32[1,1,2,512,128]{4,3,2,1,0:T(8,128)S(1)} %bitcast.611, f32[1,1,2,512,128]{4,3,2,1,0:T(8,128)S(1)} %bitcast.609, f32[]{:T(128)} %bitcast.28, f32[]{:T(128)} %bitcast.27, f32[]{:T(128)} %bitcast.25, f32[]{:T(128)} %bitcast.9, ...), kind=kLoop, calls=%fused_computation.153 | loop fusion | flops 917504 | bytes 1572896 | tf_op jit(solution)/shard_map/sub | solution.py:11
  78.7 5.1 %multiply_add_fusion.14 = (f32[1,1,1,512,128]{4,3,2,1,0:T(8,128)S(1)}, f32[1,1,1,512,128]{4,3,2,1,0:T(8,128)S(1)}) fusion(f32[1,1,2,512,128]{4,3,2,1,0:T(8,128)S(1)} %bitcast.612, f32[1,1,2,512,128]{4,3,2,1,0:T(8,128)S(1)} %bitcast.610, f32[]{:T(128)} %bitcast.28, f32[]{:T(128)} %bitcast.27, f32[]{:T(128)} %bitcast.25, f32[]{:T(128)} %bitcast.9, ...), kind=kLoop, calls=%fused_computation.152 | loop fusion | flops 917504 | bytes 1572896 | tf_op jit(solution)/shard_map/add | solution.py:12
  83.9 2.6 %subtract_bitcast_fusion.1 = (f32[1,2,256,128]{3,2,1,0:T(8,128)S(1)}, f32[1,2,256,128]{3,2,1,0:T(8,128)S(1)}) fusion(f32[2,2,2,256,128]{4,3,1,2,0:T(8,128)S(1)} %maximum_maximum_fusion, f32[]{:T(128)} %bitcast.39, f32[]{:T(128)} %bitcast.38, f32[]{:T(128)} %bitcast.37, f32[]{:T(128)} %bitcast.8), kind=kLoop, calls=%fused_computation.149 | loop fusion | flops 917504 | bytes 1572880 | tf_op jit(solution)/shard_map/sub | solution.py:11
  86.6 2.6 %subtract_bitcast_fusion = (f32[1,2,256,128]{3,2,1,0:T(8,128)S(1)}, f32[1,2,256,128]{3,2,1,0:T(8,128)S(1)}) fusion(f32[2,2,2,256,128]{4,3,1,2,0:T(8,128)S(1)} %maximum_maximum_fusion, f32[]{:T(128)} %bitcast.47, f32[]{:T(128)} %bitcast.46, f32[]{:T(128)} %bitcast.45, f32[]{:T(128)} %bitcast.44), kind=kLoop, calls=%fused_computation.147 | loop fusion | flops 917504 | bytes 1572880 | tf_op jit(solution)/shard_map/sub | solution.py:11
  89.3 2.5 %fusion.45 = f32[1,4,128,128]{3,2,1,0:T(8,128)S(1)} fusion(f32[2,4,2,128,128]{4,3,2,1,0:T(8,128)S(1)} %bitcast.590, f32[]{:T(128)} %bitcast.63, f32[]{:T(128)} %bitcast.62, f32[]{:T(128)} %bitcast.61, f32[]{:T(128)} %bitcast.60), kind=kLoop, calls=%fused_computation.131 | loop fusion | flops 458752 | bytes 1310736 | tf_op jit(solution)/shard_map/sub | solution.py:11
  91.8 2.5 %fusion.37 = f32[1,4,128,128]{3,2,1,0:T(8,128)S(1)} fusion(f32[2,4,2,128,128]{4,3,2,1,0:T(8,128)S(1)} %bitcast.591, f32[]{:T(128)} %bitcast.63, f32[]{:T(128)} %bitcast.62, f32[]{:T(128)} %bitcast.61, f32[]{:T(128)} %bitcast.60), kind=kLoop, calls=%fused_computation.119 | loop fusion | flops 458752 | bytes 1310736 | tf_op jit(solution)/shard_map/add | solution.py:12
  94.3 2.6 %fusion.40 = (f32[1,4,128,128]{3,2,1,0:T(8,128)S(1)}, f32[1,4,128,128]{3,2,1,0:T(8,128)S(1)}) fusion(f32[2,4,2,128,128]{4,3,2,1,0:T(8,128)S(1)} %bitcast.592, f32[]{:T(128)} %bitcast.54, f32[]{:T(128)} %bitcast.53, f32[]{:T(128)} %bitcast.52, f32[]{:T(128)} %bitcast.7), kind=kLoop, calls=%fused_computation.126 | loop fusion | flops 917504 | bytes 1572880 | tf_op jit(solution)/shard_map/sub | solution.py:11
  97.2 2.6 %fusion.36 = f32[1,8,64,128]{3,2,1,0:T(8,128)S(1)} fusion(f32[2,8,2,64,128]{4,3,2,1,0:T(8,128)S(1)} %bitcast.593, f32[]{:T(128)} %bitcast.83, f32[]{:T(128)} %bitcast.82, f32[]{:T(128)} %bitcast.81, f32[]{:T(128)} %bitcast.80), kind=kLoop, calls=%fused_computation.117 | loop fusion | flops 458752 | bytes 1310736 | tf_op jit(solution)/shard_map/sub | solution.py:11
  99.8 2.6 %fusion.28 = f32[1,8,64,128]{3,2,1,0:T(8,128)S(1)} fusion(f32[2,8,2,64,128]{4,3,2,1,0:T(8,128)S(1)} %bitcast.594, f32[]{:T(128)} %bitcast.83, f32[]{:T(128)} %bitcast.82, f32[]{:T(128)} %bitcast.81, f32[]{:T(128)} %bitcast.80), kind=kLoop, calls=%fused_computation.105 | loop fusion | flops 458752 | bytes 1310736 | tf_op jit(solution)/shard_map/add | solution.py:12
  102.3 2.6 %fusion.31 = (f32[1,8,64,128]{3,2,1,0:T(8,128)S(1)}, f32[1,8,64,128]{3,2,1,0:T(8,128)S(1)}) fusion(f32[2,8,2,64,128]{4,3,2,1,0:T(8,128)S(1)} %bitcast.595, f32[]{:T(128)} %bitcast.74, f32[]{:T(128)} %bitcast.73, f32[]{:T(128)} %bitcast.72, f32[]{:T(128)} %bitcast.6), kind=kLoop, calls=%fused_computation.112 | loop fusion | flops 917504 | bytes 1572880 | tf_op jit(solution)/shard_map/sub | solution.py:11
  105.3 2.6 %fusion.27 = f32[1,16,32,128]{3,2,1,0:T(8,128)S(1)} fusion(f32[2,16,2,32,128]{4,3,2,1,0:T(8,128)S(1)} %bitcast.599, f32[]{:T(128)} %bitcast.103, f32[]{:T(128)} %bitcast.102, f32[]{:T(128)} %bitcast.101, f32[]{:T(128)} %bitcast.100), kind=kLoop, calls=%fused_computation.103 | loop fusion | flops 458752 | bytes 1310736 | tf_op jit(solution)/shard_map/sub | solution.py:11
  107.9 2.6 %fusion.19 = f32[1,16,32,128]{3,2,1,0:T(8,128)S(1)} fusion(f32[2,16,2,32,128]{4,3,2,1,0:T(8,128)S(1)} %bitcast.600, f32[]{:T(128)} %bitcast.103, f32[]{:T(128)} %bitcast.102, f32[]{:T(128)} %bitcast.101, f32[]{:T(128)} %bitcast.100), kind=kLoop, calls=%fused_computation.91 | loop fusion | flops 458752 | bytes 1310736 | tf_op jit(solution)/shard_map/add | solution.py:12
  110.5 2.5 %fusion.22 = (f32[1,16,32,128]{3,2,1,0:T(8,128)S(1)}, f32[1,16,32,128]{3,2,1,0:T(8,128)S(1)}) fusion(f32[2,16,2,32,128]{4,3,2,1,0:T(8,128)S(1)} %bitcast.601, f32[]{:T(128)} %bitcast.94, f32[]{:T(128)} %bitcast.93, f32[]{:T(128)} %bitcast.92, f32[]{:T(128)} %bitcast.5), kind=kLoop, calls=%fused_computation.98 | loop fusion | flops 917504 | bytes 1572880 | tf_op jit(solution)/shard_map/sub | solution.py:11
  113.3 2.6 %fusion.18 = f32[1,32,16,128]{3,2,1,0:T(8,128)S(1)} fusion(f32[2,32,2,16,128]{4,3,2,1,0:T(8,128)S(1)} %bitcast.596, f32[]{:T(128)} %bitcast.123, f32[]{:T(128)} %bitcast.122, f32[]{:T(128)} %bitcast.121, f32[]{:T(128)} %bitcast.120), kind=kLoop, calls=%fused_computation.89 | loop fusion | flops 458752 | bytes 1310736 | tf_op jit(solution)/shard_map/sub | solution.py:11
  115.9 2.6 %fusion.10 = f32[1,32,16,128]{3,2,1,0:T(8,128)S(1)} fusion(f32[2,32,2,16,128]{4,3,2,1,0:T(8,128)S(1)} %bitcast.597, f32[]{:T(128)} %bitcast.123, f32[]{:T(128)} %bitcast.122, f32[]{:T(128)} %bitcast.121, f32[]{:T(128)} %bitcast.120), kind=kLoop, calls=%fused_computation.77 | loop fusion | flops 458752 | bytes 1310736 | tf_op jit(solution)/shard_map/add | solution.py:12
  118.4 2.7 %fusion.13 = (f32[1,32,16,128]{3,2,1,0:T(8,128)S(1)}, f32[1,32,16,128]{3,2,1,0:T(8,128)S(1)}) fusion(f32[2,32,2,16,128]{4,3,2,1,0:T(8,128)S(1)} %bitcast.598, f32[]{:T(128)} %bitcast.114, f32[]{:T(128)} %bitcast.113, f32[]{:T(128)} %bitcast.112, f32[]{:T(128)} %bitcast.4), kind=kLoop, calls=%fused_computation.84 | loop fusion | flops 917504 | bytes 1572880 | tf_op jit(solution)/shard_map/sub | solution.py:11
  121.4 2.6 %fusion.9 = f32[1,64,8,128]{3,2,1,0:T(8,128)S(1)} fusion(f32[2,64,2,8,128]{4,3,2,1,0:T(8,128)S(1)} %bitcast.602, f32[]{:T(128)} %bitcast.143, f32[]{:T(128)} %bitcast.142, f32[]{:T(128)} %bitcast.141, f32[]{:T(128)} %bitcast.140), kind=kLoop, calls=%fused_computation.75 | loop fusion | flops 458752 | bytes 1310736 | tf_op jit(solution)/shard_map/sub | solution.py:11
  124.0 2.6 %fusion.1 = f32[1,64,8,128]{3,2,1,0:T(8,128)S(1)} fusion(f32[2,64,2,8,128]{4,3,2,1,0:T(8,128)S(1)} %bitcast.603, f32[]{:T(128)} %bitcast.143, f32[]{:T(128)} %bitcast.142, f32[]{:T(128)} %bitcast.141, f32[]{:T(128)} %bitcast.140), kind=kLoop, calls=%fused_computation.63 | loop fusion | flops 458752 | bytes 1310736 | tf_op jit(solution)/shard_map/add | solution.py:12
  126.6 2.7 %fusion.4 = (f32[1,64,8,128]{3,2,1,0:T(8,128)S(1)}, f32[1,64,8,128]{3,2,1,0:T(8,128)S(1)}) fusion(f32[2,64,2,8,128]{4,3,2,1,0:T(8,128)S(1)} %bitcast.604, f32[]{:T(128)} %bitcast.134, f32[]{:T(128)} %bitcast.133, f32[]{:T(128)} %bitcast.132, f32[]{:T(128)} %bitcast.3), kind=kLoop, calls=%fused_computation.70 | loop fusion | flops 917504 | bytes 1572880 | tf_op jit(solution)/shard_map/sub | solution.py:11
  129.7 2.6 %multiply_subtract_fusion.12 = (f32[1,128,512]{2,1,0:T(8,128)S(1)}, f32[1,128,512]{2,1,0:T(8,128)S(1)}) fusion(f32[2,128,1024]{2,1,0:T(8,128)S(1)} %reshape_reshape.32, f32[]{:T(128)} %bitcast.153, f32[]{:T(128)} %bitcast.152, f32[]{:T(128)} %bitcast.151, f32[]{:T(128)} %bitcast.2), kind=kLoop, calls=%fused_computation.145 | loop fusion | flops 917504 | bytes 1572880 | tf_op jit(solution)/shard_map/sub | solution.py:11
  132.3 2.6 %multiply_subtract_fusion.11 = (f32[1,128,512]{2,1,0:T(8,128)S(1)}, f32[1,128,512]{2,1,0:T(8,128)S(1)}) fusion(f32[2,128,1024]{2,1,0:T(8,128)S(1)} %reshape_reshape.32, f32[]{:T(128)} %bitcast.157, f32[]{:T(128)} %bitcast.156, f32[]{:T(128)} %bitcast.155, f32[]{:T(128)} %bitcast.154), kind=kLoop, calls=%fused_computation.143 | loop fusion | flops 917504 | bytes 1572880 | tf_op jit(solution)/shard_map/sub | solution.py:11
  135.2 2.4 %multiply_subtract_fusion.10 = (f32[1,256,256]{2,1,0:T(8,128)S(1)}, f32[1,256,256]{2,1,0:T(8,128)S(1)}) fusion(f32[2,256,512]{2,1,0:T(8,128)S(1)} %reshape_reshape.33, f32[]{:T(128)} %bitcast.160, f32[]{:T(128)} %bitcast.159, f32[]{:T(128)} %bitcast.158, f32[]{:T(128)} %bitcast.1), kind=kLoop, calls=%fused_computation.141 | loop fusion | flops 917504 | bytes 1572880 | tf_op jit(solution)/shard_map/sub | solution.py:11
  137.6 2.6 %multiply_subtract_fusion.9 = (f32[1,256,256]{2,1,0:T(8,128)S(1)}, f32[1,256,256]{2,1,0:T(8,128)S(1)}) fusion(f32[2,256,512]{2,1,0:T(8,128)S(1)} %reshape_reshape.33, f32[]{:T(128)} %bitcast.164, f32[]{:T(128)} %bitcast.163, f32[]{:T(128)} %bitcast.162, f32[]{:T(128)} %bitcast.161), kind=kLoop, calls=%fused_computation.139 | loop fusion | flops 917504 | bytes 1572880 | tf_op jit(solution)/shard_map/sub | solution.py:11
  140.6 2.6 %multiply_subtract_fusion.8 = (f32[1,512,128]{2,1,0:T(8,128)S(1)}, f32[1,512,128]{2,1,0:T(8,128)S(1)}) fusion(f32[2,512,256]{2,1,0:T(8,128)S(1)} %reshape_reshape.34, f32[]{:T(128)} %bitcast.167, f32[]{:T(128)} %bitcast.166, f32[]{:T(128)} %bitcast.165, f32[]{:T(128)} %bitcast), kind=kLoop, calls=%fused_computation.137 | loop fusion | flops 917504 | bytes 1572880 | tf_op jit(solution)/shard_map/sub | solution.py:11
  143.2 2.6 %multiply_subtract_fusion.7 = (f32[1,512,128]{2,1,0:T(8,128)S(1)}, f32[1,512,128]{2,1,0:T(8,128)S(1)}) fusion(f32[2,512,256]{2,1,0:T(8,128)S(1)} %reshape_reshape.34, f32[]{:T(128)} %bitcast.171, f32[]{:T(128)} %bitcast.170, f32[]{:T(128)} %bitcast.169, f32[]{:T(128)} %bitcast.168), kind=kLoop, calls=%fused_computation.135 | loop fusion | flops 917504 | bytes 1572880 | tf_op jit(solution)/shard_map/sub | solution.py:11
  153.2 10.7 %stack.323 = f32[20]{0:T(128)S(1)} concatenate(f32[1]{0:T(128)} %bitcast.212, f32[1]{0:T(128)} %bitcast.213, f32[1]{0:T(128)} %bitcast.214, f32[1]{0:T(128)} %bitcast.215, f32[1]{0:T(128)} %bitcast.216, f32[1]{0:T(128)} %bitcast.217, f32[1]{0:T(128)} %bitcast.218, f32[1]{0:T(128)} %bitcast.219, f32[1]{0:T(128)} %bitcast.220, f32[1]{0:T(128)} %bitcast.221, f32[1]{0:T(128)} %bitcast.222, ...), dimensions={0} | concatenate | bytes 160 | tf_op jit(solution)/shard_map/stack | solution.py:101
  163.9 3.3 %add.1087 = s32[1024,1,128]{2,1,0:T(1,128)S(1)} broadcast(s32[1024]{0:T(1024)S(1)} %multiply_add_fusion.17), dimensions={0} | broadcast | bytes 528384 | tf_op jit(solution)/shard_map/add | solution.py:54
  167.3 0.9 subtract_convert_fusion.1
  168.2 20.8 %psum.7 = f32[20]{0:T(128)S(1)} all-reduce(f32[20]{0:T(128)S(1)} %stack.323), channel_id=1, replica_groups=mesh['q'=8] {'q'}, use_global_device_ids=true, to_apply=%region_20.21 | all-reduce | flops 20 | bytes 160 | tf_op jit(solution)/shard_map/psum | solution.py:101
  189.5 2.1 %maximum_multiply_fusion = f32[2,131072]{1,0:T(2,128)} fusion(f32[1,131072]{1,0:T(1,128)S(1)} %bitcast.608, f32[1,131072]{1,0:T(1,128)S(1)} %bitcast.606, f32[131072]{0:T(1024)S(1)} %subtract_convert_fusion.1), kind=kLoop, calls=%fused_computation.17 | loop fusion | flops 524288 | bytes 2621440 | tf_op jit(solution)/shard_map/mul | solution.py:96
  (90 shorter events, 19.2 us)
Async XLA Ops:
  1.9 25.0 %collective-permute-start = (f32[2,1024,128]{2,1,0:T(8,128)S(1)}, f32[2,1024,128]{2,1,0:T(8,128)S(1)}, u32[]{:S(2)}, u32[]{:S(2)}) collective-permute-start(f32[2,1024,128]{2,1,0:T(8,128)S(1)} %bitcast.617), channel_id=1, source_target_pairs={{0,4},{1,5},{2,6},{3,7},{4,0},{5,1},{6,2},{7,3}} | collective-permute-start | bytes 3145736 | tf_op jit(solution)/shard_map/ppermute | solution.py:86
  29.4 30.3 %collective-permute-start.1 = (f32[2,1024,128]{2,1,0:T(8,128)}, f32[2,1024,128]{2,1,0:T(8,128)}, u32[]{:S(2)}, u32[]{:S(2)}) collective-permute-start(f32[2,1024,128]{2,1,0:T(8,128)} %pad_maximum_fusion), channel_id=1, source_target_pairs={{0,2},{1,3},{2,0},{3,1},{4,6},{5,7},{6,4},{7,5}} | collective-permute-start | bytes 3145736 | tf_op jit(solution)/shard_map/ppermute | solution.py:86
  36.3 8.2 %copy-start = (s32[10,2]{0,1:T(2,128)S(1)}, s32[10,2]{0,1:T(2,128)}, u32[]{:S(2)}) copy-start(s32[10,2]{0,1:T(2,128)} %param.5) | copy-start | bytes 244
  63.8 6.9 %collective-permute-start.2 = (f32[2,1024,128]{2,1,0:T(8,128)S(1)}, f32[2,1024,128]{2,1,0:T(8,128)S(1)}, u32[]{:S(2)}, u32[]{:S(2)}) collective-permute-start(f32[2,1024,128]{2,1,0:T(8,128)S(1)} %pad_maximum_fusion.1), channel_id=1, source_target_pairs={{0,1},{1,0},{2,3},{3,2},{4,5},{5,4},{6,7},{7,6}} | collective-permute-start | bytes 3145736 | tf_op jit(solution)/shard_map/ppermute | solution.py:86
where the time goes:
time: 195 us; the launch traced here: 192 us
  other arithmetic  96.8 us (50%)
  local copies, waits for them, and re-layouts  39.2 us (20%)
  blocking collectives  20.8 us (11%)
  between operations  16.4 us (8%)
  waiting for transfers between devices  11.1 us (6%)
  starting transfers between devices  5.07 us (3%)
  matrix products  2.26 us (1%)
    sub x22, other arithmetic, mix_pair(): coef_a[0] * first[0] - coef_a[1] * first[1] + coef_b[0] * second[0]  60.1 us
    add x7, other arithmetic, mix_pair(): coef_a[0] * first[1] + coef_a[1] * first[0] + coef_b[0] * second[1]  21.9 us
    psum x1, blocking collectives, local_layer(): lax.psum(jnp.stack(top_part + low_part), 'q') / (local_size * group_size)  20.8 us
    ppermute x3, waiting for transfers between devices, local_layer(): lax.ppermute(grid, 'q', [(source, source ^ flip_mask) for source in range...  11.1 us
    another operation x1, local copies, waits for them, and re-layouts, local_layer(): jnp.stack(top_part + low_part)  10.7 us
    add x7, local copies, waits for them, and re-layouts, low_block(): block_re[:, None, :, None] * tr_im[None, :, None, :]  6.26 us
    sub x7, other arithmetic, low_block(): block_re[:, None, :, None] * tr_re[None, :, None, :]  5.41 us
    slice x8, local copies, waits for them, and re-layouts, mix_pair(): coef_a[0] * first[0] - coef_a[1] * first[1] + coef_b[0] * second[0]  5.16 us
  transfers between devices with their start and end apart: 3, of which 1 were waited for; matrix products, arithmetic and copies ran while one was open for 17% of the time, Pallas kernels for 0%

commit v1 on v0

v1 whole, which is shorter than its diff:
```python
import jax
import jax.numpy as jnp
from jax import lax
from jax.experimental import pallas as pl
from jax.experimental.pallas import tpu as pltpu
from jax.sharding import PartitionSpec as P

MESH = pl.DeviceIdType.MESH
F32 = jnp.float32
ROWS = 128
CHUNK = 2 * ROWS
CHUNKS = 4
PIECES = 4
PROWS = ROWS // PIECES
DEVICES = 8


def cmul2(coef_a, first, coef_b, second):
    re = coef_a[0] * first[0] - coef_a[1] * first[1] + coef_b[0] * second[0] - coef_b[1] * second[1]
    im = coef_a[0] * first[1] + coef_a[1] * first[0] + coef_b[0] * second[1] + coef_b[1] * second[0]
    return re, im


def kernel(X, u_ref, cz_ref, OUT, z_ref,
           RB, XP, RP, S, R2, T, SG, GM, KM, XC, ZC, TP, V, VR,
           s1s, s1r, cps, cpr, fws, fwr, s2s, s2r, zs, zr):
    me = lax.axis_index('q')
    bit_y = me // 4
    bit_x = (me // 2) % 2
    bit_c = me % 2
    dev_y = me + 4 * (1 - 2 * bit_y)
    dev_x = me + 2 * (1 - 2 * bit_x)
    dev_c = me + (1 - 2 * bit_c)
    first_dev = (dev_x, dev_y)
    second_dev = (dev_y, dev_x)

    def remote(src, dst, send, recv, dev):
        return pltpu.make_async_remote_copy(src_ref=src, dst_ref=dst, send_sem=send, recv_sem=recv,
                                            device_id=(dev,), device_id_type=MESH)

    def stage1(half, chunk):
        k = half * CHUNKS + chunk
        rows = pl.ds(k * CHUNK, CHUNK)
        return remote(X.at[rows], RB.at[rows], s1s.at[k], s1r.at[k], first_dev[half])

    def core_copy(half, chunk):
        k = half * CHUNKS + chunk
        rows = pl.ds(k * CHUNK, CHUNK)
        return remote(X.at[rows], XP.at[rows], cps.at[k], cpr.at[k], dev_c)

    def forward(half, chunk):
        k = half * CHUNKS + chunk
        rows = pl.ds(k * CHUNK, CHUNK)
        return remote(RB.at[rows], RP.at[rows], fws.at[k], fwr.at[k], dev_c)

    def stage2(half, chunk, piece):
        k = (half * CHUNKS + chunk) * PIECES + piece
        rows = pl.ds(piece * PROWS, PROWS)
        return remote(S.at[half, chunk, :, rows], R2.at[half, chunk, :, rows], s2s.at[k], s2r.at[k], second_dev[half])

    barrier = pltpu.get_barrier_semaphore()
    for dev in (dev_x, dev_y, dev_c):
        pl.semaphore_signal(barrier, inc=1, device_id=(dev,), device_id_type=MESH)
    pl.semaphore_wait(barrier, 3)

    for chunk in range(CHUNKS):
        for half in range(2):
            stage1(half, chunk).start()
    for chunk in range(CHUNKS):
        for half in range(2):
            core_copy(half, chunk).start()

    def entry(qubit, row, col):
        return u_ref[row * 2 + col, qubit], u_ref[4 + row * 2 + col, qubit]

    lane = lax.broadcasted_iota(jnp.int32, (8, 128), 1)
    sub = lax.broadcasted_iota(jnp.int32, (8, 128), 0)

    def build(t, carry):
        row = sub + 8 * t
        for base, left in ((6, True), (13, False)):
            re = im = None
            for j in range(7):
                shift = 6 - j
                row_bit = ((row >> shift) & 1) == 1
                col_bit = ((lane >> shift) & 1) == 1
                fac = []
                for ri in range(2):
                    u00, u01, u10, u11 = [u_ref[4 * ri + k, base + j] for k in range(4)]
                    if not left:
                        u01, u10 = u10, u01
                    fac.append(jnp.where(row_bit, jnp.where(col_bit, u11, u10), jnp.where(col_bit, u01, u00)))
                if re is None:
                    re, im = fac
                else:
                    re, im = re * fac[0] - im * fac[1], re * fac[1] + im * fac[0]
            low = pl.ds(pl.multiple_of(8 * t, 8), 8)
            high = pl.ds(pl.multiple_of(128 + 8 * t, 8), 8)
            if left:
                GM[low, 0:128] = re
                GM[low, 128:256] = -im
                GM[high, 0:128] = im
                GM[high, 128:256] = re
            else:
                KM[low, 0:128] = re
                KM[low, 128:256] = im
                KM[high, 0:128] = -im
                KM[high, 128:256] = re
        return carry

    lax.fori_loop(0, 16, build, 0)

    num_pairs = cz_ref.shape[1]
    shifts = [(19 - cz_ref[0, k], 19 - cz_ref[1, k]) for k in range(num_pairs)]

    def build_signs(t, carry):
        flat = me * 131072 + (sub + 8 * t) * 128 + lane
        parity = jnp.zeros_like(flat)
        for shift_a, shift_b in shifts:
            parity = parity ^ ((flat >> shift_a) & (flat >> shift_b))
        SG[pl.ds(pl.multiple_of(8 * t, 8), 8), :] = (1 - 2 * (parity & 1)).astype(F32)
        return carry

    lax.fori_loop(0, 128, build_signs, 0)

    def gate_pair(qubit, own_bit):
        return entry(qubit, own_bit, own_bit), entry(qubit, own_bit, 1 - own_bit)

    def scalar_mul(a, b):
        return a[0] * b[0] - a[1] * b[1], a[0] * b[1] + a[1] * b[0]

    coef_y = gate_pair(0, bit_y)
    coef_x = gate_pair(1, bit_x)
    coef_c = gate_pair(2, bit_c)
    stage1_coefs = []
    for coef in (coef_x, coef_y):
        stage1_coefs.append([scalar_mul(coef[0], coef_c[0]), scalar_mul(coef[1], coef_c[0]),
                             scalar_mul(coef[0], coef_c[1]), scalar_mul(coef[1], coef_c[1])])

    for chunk in range(CHUNKS):
        for half in range(2):
            stage1(half, chunk).wait_recv()
            forward(half, chunk).start()
        if chunk:
            for piece in range(PIECES):
                for half in range(2):
                    stage2(half, chunk - 1, piece).start()
        for half in range(2):
            core_copy(half, chunk).wait_recv()
            forward(half, chunk).wait_recv()

        for half in range(2):
            coefs = stage1_coefs[half]
            base = (half * CHUNKS + chunk) * CHUNK

            def combine(t, carry, base=base, coefs=coefs, half=half):
                at = pl.multiple_of(base + 16 * t, 16)
                re = im = None
                for ref, coef in zip((X, RB, XP, RP), coefs):
                    a = ref[pl.ds(at, 8, stride=2), :]
                    b = ref[pl.ds(at + 1, 8, stride=2), :]
                    part_re = coef[0] * a - coef[1] * b
                    part_im = coef[0] * b + coef[1] * a
                    re = part_re if re is None else re + part_re
                    im = part_im if im is None else im + part_im
                XC[pl.ds(pl.multiple_of(8 * t, 8), 8), half * 128:half * 128 + 128] = re
                XC[pl.ds(pl.multiple_of(128 + 8 * t, 8), 8), half * 128:half * 128 + 128] = im
                return carry

            lax.fori_loop(0, 16, combine, 0, unroll=2)
        left = lax.dot(GM[...], XC[...], precision=lax.Precision.HIGHEST, preferred_element_type=F32)
        ZC[0:128, 0:128] = left[0:128, 0:128]
        ZC[0:128, 128:256] = left[128:256, 0:128]
        ZC[128:256, 0:128] = left[0:128, 128:256]
        ZC[128:256, 128:256] = left[128:256, 128:256]
        both = lax.dot(ZC[...], KM[...], precision=lax.Precision.HIGHEST, preferred_element_type=F32)
        S[0, chunk, 0] = both[0:128, 0:128]
        S[0, chunk, 1] = both[0:128, 128:256]
        S[1, chunk, 0] = both[128:256, 0:128]
        S[1, chunk, 1] = both[128:256, 128:256]

    u3 = [entry(3, 0, 0), entry(3, 0, 1), entry(3, 1, 0), entry(3, 1, 1)]
    u4 = [entry(4, 0, 0), entry(4, 0, 1), entry(4, 1, 0), entry(4, 1, 1)]
    u5 = [entry(5, 0, 0), entry(5, 0, 1), entry(5, 1, 0), entry(5, 1, 1)]

    def gate(mat, zero, one):
        return cmul2(mat[0], zero, mat[1], one), cmul2(mat[2], zero, mat[3], one)

    def second_gate(chunk, rows):
        def pair(ref, half):
            return ref[half, chunk, 0, rows, :], ref[half, chunk, 1, rows, :]
        zero = cmul2(coef_y[0], pair(S, 0), coef_y[1], pair(R2, 0))
        one = cmul2(coef_x[0], pair(S, 1), coef_x[1], pair(R2, 1))
        return gate(u3, zero, one)

    def read(half, chunk, rows):
        return T[half, chunk, 0, rows, :], T[half, chunk, 1, rows, :]

    def keep(half, chunk, rows, value):
        T[half, chunk, 0, rows, :] = value[0]
        T[half, chunk, 1, rows, :] = value[1]

    def piece_rows(t):
        return pl.ds(pl.multiple_of(8 * t, 8), 8)

    def step_even(chunk):
        def body(t, carry):
            rows = piece_rows(t)
            both = second_gate(chunk, rows)
            for half in range(2):
                keep(half, chunk, rows, both[half])
            return carry
        return body

    def step_odd(t, carry):
        rows = piece_rows(t)
        both = second_gate(1, rows)
        for half in range(2):
            zero, one = gate(u5, read(half, 0, rows), both[half])
            keep(half, 0, rows, zero)
            keep(half, 1, rows, one)
        return carry

    def step_last(t, sums):
        rows = piece_rows(t)
        both = second_gate(3, rows)
        sums = list(sums)
        total = None
        for half in range(2):
            two, three = gate(u5, read(half, 2, rows), both[half])
            out_0, out_2 = gate(u4, read(half, 0, rows), two)
            out_1, out_3 = gate(u4, read(half, 1, rows), three)
            for chunk, value in enumerate((out_0, out_1, out_2, out_3)):
                block = half * CHUNKS + chunk
                sign = SG[pl.ds(pl.multiple_of(block * ROWS + 8 * t, 8), 8), :]
                re, im = value[0] * sign, value[1] * sign
                at = pl.multiple_of(block * CHUNK + 16 * t, 16)
                OUT[pl.ds(at, 8, stride=2), :] = re
                OUT[pl.ds(at + 1, 8, stride=2), :] = im
                density = re * re + im * im
                sums[block] = sums[block] + density
                total = density if total is None else total + density
        TP[pl.ds(pl.multiple_of(8 * t, 8), 8), :] = total
        return tuple(sums)

    per_piece = PROWS // 8
    sums = tuple(jnp.zeros((8, 128), F32) for _ in range(8))
    for chunk in range(CHUNKS):
        for piece in range(PIECES):
            for half in range(2):
                stage2(half, chunk, piece).wait_recv()
            if chunk == 0 and piece == 0:
                for other in range(PIECES):
                    for half in range(2):
                        stage2(half, CHUNKS - 1, other).start()
            span = (piece * per_piece, (piece + 1) * per_piece)
            if chunk == 3:
                sums = lax.fori_loop(*span, step_last, sums)
            elif chunk == 1:
                lax.fori_loop(*span, step_odd, 0)
            else:
                lax.fori_loop(*span, step_even(chunk), 0)

    def signed(parts, bit):
        acc = None
        for index, part in enumerate(parts):
            if acc is None:
                acc = part
            elif (index >> bit) & 1:
                acc = acc - part
            else:
                acc = acc + part
        return acc

    def fold(part):
        return jnp.sum(part, axis=0, keepdims=True)

    parts = [TP[8 * t:8 * t + 8, :] for t in range(16)]
    total = signed(parts, 10)
    tot_row = fold(total)
    rows = [tot_row] * 3
    rows += [fold(signed(sums, bit)) for bit in (2, 1, 0)]
    rows += [fold(signed(parts, bit)) for bit in (3, 2, 1, 0)]
    rows += [fold(total * (1 - 2 * ((sub >> bit) & 1)).astype(F32)) for bit in (2, 1, 0)]
    lane_row = lane[0:1, :]
    rows += [tot_row * (1 - 2 * ((lane_row >> bit) & 1)).astype(F32) for bit in (6, 5, 4, 3, 2, 1, 0)]
    rows += [jnp.zeros((1, 128), F32)] * 4
    mine = jnp.concatenate(rows, axis=0)
    V[...] = mine

    def z_copy(dist):
        flip_y, flip_x, flip_c = dist // 4, (dist // 2) % 2, dist % 2
        dev = (me + 4 * flip_y * (1 - 2 * bit_y) + 2 * flip_x * (1 - 2 * bit_x) + flip_c * (1 - 2 * bit_c))
        return remote(V, VR.at[dist], zs.at[dist], zr.at[dist], dev)

    for dist in (7, 6, 5, 3, 4, 2, 1):
        z_copy(dist).start()

    for chunk in range(CHUNKS):
        for half in range(2):
            stage1(half, chunk).wait_send()
            core_copy(half, chunk).wait_send()
            forward(half, chunk).wait_send()
            for piece in range(PIECES):
                stage2(half, chunk, piece).wait_send()

    row24 = lax.broadcasted_iota(jnp.int32, (24, 128), 0)
    col24 = lax.broadcasted_iota(jnp.int32, (24, 128), 1)
    own_sign = jnp.where(row24 == 0, 1 - 2 * bit_y, jnp.where(row24 == 1, 1 - 2 * bit_x, jnp.where(row24 == 2, 1 - 2 * bit_c, 1))).astype(F32)
    acc = mine
    for dist in (1, 2, 4, 3, 5, 6, 7):
        z_copy(dist).wait_recv()
        value = VR[dist]
        flips = [k for k, bit in ((0, 4), (1, 2), (2, 1)) if dist & bit]
        mask = row24 == flips[0]
        for k in flips[1:]:
            mask = mask | (row24 == k)
        acc = acc + jnp.where(mask, -value, value)
    acc = acc * own_sign
    column = jnp.sum(acc, axis=1, keepdims=True)
    spread = jnp.where(row24 == col24, column, 0.0)
    z_ref[...] = jnp.sum(spread, axis=0, keepdims=True)[:, 0:20] * (1.0 / (131072 * DEVICES))
    for dist in range(1, DEVICES):
        z_copy(dist).wait_send()


def solution(mesh):
    def local_layer(state_local, unitaries, cz_pairs):
        size = state_local.shape[1]
        rows = 2 * size // 128
        x = state_local.reshape(2, size // 128, 128).transpose(1, 0, 2).reshape(rows, 128)
        u = unitaries.transpose(0, 2, 3, 1).reshape(8, 20)
        cz = cz_pairs.T
        vm = pltpu.VMEM
        dma = pltpu.SemaphoreType.DMA
        out, z = pl.pallas_call(
            kernel,
            out_shape=(jax.ShapeDtypeStruct((rows, 128), F32), jax.ShapeDtypeStruct((1, 20), F32)),
            in_specs=[pl.BlockSpec(memory_space=pltpu.VMEM), pl.BlockSpec(memory_space=pltpu.SMEM), pl.BlockSpec(memory_space=pltpu.SMEM)],
            out_specs=(pl.BlockSpec(memory_space=pltpu.VMEM), pl.BlockSpec(memory_space=pltpu.VMEM)),
            scratch_shapes=[
                vm((rows, 128), F32), vm((rows, 128), F32), vm((rows, 128), F32),
                vm((2, CHUNKS, 2, ROWS, 128), F32), vm((2, CHUNKS, 2, ROWS, 128), F32), vm((2, CHUNKS, 2, ROWS, 128), F32),
                vm((rows // 2, 128), F32),
                vm((256, 256), F32), vm((256, 256), F32), vm((256, 256), F32), vm((256, 256), F32),
                vm((128, 128), F32), vm((24, 128), F32), vm((DEVICES, 24, 128), F32),
                dma((8,)), dma((8,)), dma((8,)), dma((8,)), dma((8,)), dma((8,)),
                dma((8 * PIECES,)), dma((8 * PIECES,)), dma((DEVICES,)), dma((DEVICES,)),
            ],
            compiler_params=pltpu.CompilerParams(collective_id=0, has_side_effects=True, vmem_limit_bytes=40 * 2 ** 20),
        )(x, u, cz)
        state = out.reshape(size // 128, 2, 128).transpose(1, 0, 2).reshape(2, size)
        return state, z.reshape(20)

    return jax.shard_map(local_layer, mesh=mesh, in_specs=(P(None, 'q'), P(), P()), out_specs=(P(None, 'q'), P()), check_vma=False)
```

time: 195 us -> 37.3 us (0.19)
  the two profiles are of different devices: /device:TPU:1 before, /device:TPU:0 now
where the time goes in v1:
time: 37.3 us; the launch traced here: 37.2 us
  Pallas kernels  33.1 us (89%)
  local copies, waits for them, and re-layouts  3.39 us (9%)
  between operations  0.66 us (2%)
    pallas_call x1, Pallas kernels, local_layer(): pl.pallas_call(kernel, out_shape=(jax.ShapeDtypeStruct((rows, 128), F32),...  33.1 us
    unnamed x8, local copies, waits for them, and re-layouts  3.39 us

profile of v1, /device:TPU:0, one launch (start us, length us, event | category | flops | bytes accessed | tf_op | source)
XLA Modules:
  0.0 37.2 jit_solution(18357069478971355119)
XLA Ops:
  0.6 0.0 copy-start.1
  0.6 0.0 copy-start.2
  0.6 0.7 %copy-done.1 = f32[2,20,2,2]{1,3,2,0:T(2,128)S(1)} copy-done((f32[2,20,2,2]{1,3,2,0:T(2,128)S(1)}, f32[2,20,2,2]{1,3,2,0:T(2,128)}, u32[]{:S(2)}) %copy-start.1) | copy-done | bytes 664
  1.3 0.0 copy-done.2
  1.3 0.0 copy-start
  1.3 1.2 %copy-done = f32[2,131072]{1,0:T(2,128)S(1)} copy-done((f32[2,131072]{1,0:T(2,128)S(1)}, f32[2,131072]{1,0:T(2,128)}, u32[]{:S(2)}) %copy-start) | copy-done | bytes 1048600
  2.6 33.1 %shard_map.50 = (f32[2048,128]{1,0:T(8,128)S(1)}, f32[1,20]{1,0:T(1,128)S(1)}) custom-call(f32[2048,128]{1,0:T(8,128)S(1)} %bitcast.15, f32[8,20]{1,0:T(8,128)S(1)} %bitcast.17, s32[2,10]{1,0:T(2,128)S(1)} %bitcast.18), custom_call_target="tpu_custom_call" | custom-call | tf_op jit(solution)/shard_map/pallas_call | solution.py:336
  35.7 1.0 %copy.9 = f32[2,131072]{1,0:T(2,128)} copy(f32[2,131072]{1,0:T(2,128)S(1)} %bitcast.16) | data formatting | bytes 2097152
  36.6 0.5 %copy.10 = f32[20]{0:T(128)} copy(f32[20]{0:T(128)S(1)} %bitcast.19) | data formatting | bytes 160
Async XLA Ops:
  0.6 0.7 %copy-start.1 = (f32[2,20,2,2]{1,3,2,0:T(2,128)S(1)}, f32[2,20,2,2]{1,3,2,0:T(2,128)}, u32[]{:S(2)}) copy-start(f32[2,20,2,2]{1,3,2,0:T(2,128)} %param.4) | copy-start | bytes 1924
  0.6 0.7 %copy-start.2 = (s32[10,2]{0,1:T(2,128)S(1)}, s32[10,2]{0,1:T(2,128)}, u32[]{:S(2)}) copy-start(s32[10,2]{0,1:T(2,128)} %param.5) | copy-start | bytes 244
  1.3 1.2 %copy-start = (f32[2,131072]{1,0:T(2,128)S(1)}, f32[2,131072]{1,0:T(2,128)}, u32[]{:S(2)}) copy-start(f32[2,131072]{1,0:T(2,128)} %param.3) | copy-start | bytes 3145732

commit v2 on v0

v2 whole, which is shorter than its diff:
```python
import jax
import jax.numpy as jnp
from jax import lax
from jax.experimental import pallas as pl
from jax.experimental.pallas import tpu as pltpu
from jax.sharding import PartitionSpec as P

MESH = pl.DeviceIdType.MESH
F32 = jnp.float32
LANES = 128
SUB = 8
TILES = 16
LOW, HIGH = slice(0, LANES), slice(LANES, 2 * LANES)
ROWS = SUB * TILES
CHUNK = 2 * ROWS
CHUNKS = 4
PIECES = (0, 48, 88, 112, 128)
EARLY = 2
DEVICES = 8
QUBITS = 20
scope = jax.named_scope


def cmul(a, b):
    (a_re, a_im), (b_re, b_im) = a, b
    return a_re * b_re - a_im * b_im, a_re * b_im + a_im * b_re


def cadd(a, b):
    (a_re, a_im), (b_re, b_im) = a, b
    return a_re + b_re, a_im + b_im


def conj_mul(a, b):
    (a_re, a_im), (b_re, b_im) = a, b
    return a_re * b_re + a_im * b_im, a_re * b_im - a_im * b_re


def mix(coefs, values):
    total = None
    for coef, value in zip(coefs, values):
        part = cmul(coef, value)
        total = part if total is None else cadd(total, part)
    return total


def gate(mat, zero, one):
    u00, u01, u10, u11 = mat
    return mix((u00, u01), (zero, one)), mix((u10, u11), (zero, one))


def norm(a):
    re, im = a
    return re * re + im * im


def plus_minus(bit):
    return 1 - 2 * bit


def planes(ref, half, chunk, rows):
    return [ref[half, chunk, part, rows, :] for part in range(2)]


def put(ref, half, chunk, rows, value):
    for part in range(2):
        ref[half, chunk, part, rows, :] = value[part]


def tile(t, first=0):
    return pl.ds(pl.multiple_of(first + SUB * t, SUB), SUB)


def kernel(x_hbm, u_hbm, cz_hbm, OUT, z_ref,
           X, u_ref, cz_ref, RB, XP, RP, S, R2, T, SG, GM, KM, XC, ZC, TP, V, VR,
           ld, s1s, s1r, cps, cpr, fws, fwr, s2s, s2r, zs, zr):
    me = lax.axis_index('q')
    bit_y = me // 4
    bit_x = (me // 2) % 2
    bit_c = me % 2
    step_y, step_x, step_c = 4 * plus_minus(bit_y), 2 * plus_minus(bit_x), plus_minus(bit_c)
    dev_y, dev_x, dev_c = me + step_y, me + step_x, me + step_c
    first_dev = (dev_x, dev_y)
    second_dev = (dev_y, dev_x)
    second_bit = (bit_y, bit_x)

    def sent(half, k):
        return k + second_bit[half] * (3 - 2 * k)

    def received(half, k):
        return 3 - k + second_bit[half] * (2 * k - 3)

    def block_rows(half, chunk):
        return pl.ds(pl.multiple_of((half * CHUNKS + chunk) * CHUNK, CHUNK), CHUNK)

    def remote(src, dst, send, recv, dev):
        return pltpu.make_async_remote_copy(src_ref=src, dst_ref=dst, send_sem=send, recv_sem=recv,
                                            device_id=(dev,), device_id_type=MESH)

    def wait_bytes(ref, sem):
        pltpu.make_async_copy(ref, ref, sem).wait()

    def load_copy(half, k):
        rows = block_rows(half, sent(half, k))
        return pltpu.make_async_copy(x_hbm.at[rows], X.at[rows], ld.at[min(k, 1)])

    def stage1(half, k):
        rows = block_rows(half, sent(half, k))
        return remote(X.at[rows], RB.at[rows], s1s, s1r.at[k], first_dev[half])

    def core_copy(half, k):
        rows = block_rows(half, sent(half, k))
        return remote(X.at[rows], XP.at[rows], cps, cpr, dev_c)

    def forward(half, k):
        rows = block_rows(half, sent(half, k))
        return remote(RB.at[rows], RP.at[rows], fws, fwr.at[k], dev_c)

    def stage2(half, k, piece=None):
        chunk = sent(half, k)
        if piece is None:
            return remote(S.at[half, chunk], R2.at[half, chunk], s2s, s2r.at[k], second_dev[half])
        rows = pl.ds(PIECES[piece], PIECES[piece + 1] - PIECES[piece])
        return remote(S.at[half, chunk, :, rows], R2.at[half, chunk, :, rows], s2s, s2r.at[3 + piece], second_dev[half])

    u_copy = pltpu.make_async_copy(u_hbm, u_ref, ld.at[2])
    cz_copy = pltpu.make_async_copy(cz_hbm, cz_ref, ld.at[3])
    for k in range(CHUNKS):
        for half in range(2):
            load_copy(half, k).start()
    u_copy.start()
    cz_copy.start()

    barrier = pltpu.get_barrier_semaphore()
    for dev in (dev_x, dev_y, dev_c):
        pl.semaphore_signal(barrier, inc=1, device_id=(dev,), device_id_type=MESH)
    with scope('bar'):
        pl.semaphore_wait(barrier, 3)

    with scope('w_ld'):
        wait_bytes(X.at[0:2 * CHUNK], ld.at[0])
    for half in range(2):
        stage1(half, 0).start()
    with scope('w_ld'):
        wait_bytes(X.at[0:6 * CHUNK], ld.at[1])
    for k in range(1, CHUNKS):
        for half in range(2):
            stage1(half, k).start()
    for k in range(CHUNKS):
        for half in range(2):
            core_copy(half, k).start()
    u_copy.wait()
    cz_copy.wait()

    def entry(qubit, row, col):
        return u_ref[row * 2 + col, qubit], u_ref[4 + row * 2 + col, qubit]

    def matrix(qubit, flip=0):
        return [entry(qubit, row + flip * plus_minus(row), col + flip * plus_minus(col)) for row in range(2) for col in range(2)]

    lane = lax.broadcasted_iota(jnp.int32, (SUB, LANES), 1)
    sub = lax.broadcasted_iota(jnp.int32, (SUB, LANES), 0)

    def build(t, carry):
        row = sub + SUB * t
        for base, left in ((6, True), (13, False)):
            re = im = None
            for j in range(7):
                shift = 6 - j
                row_bit = ((row >> shift) & 1) == 1
                col_bit = ((lane >> shift) & 1) == 1
                fac = []
                for ri in range(2):
                    u00, u01, u10, u11 = [u_ref[4 * ri + k, base + j] for k in range(4)]
                    if not left:
                        u01, u10 = u10, u01
                    fac.append(jnp.where(row_bit, jnp.where(col_bit, u11, u10), jnp.where(col_bit, u01, u00)))
                if re is None:
                    re, im = fac
                else:
                    re, im = cmul((re, im), fac)
            low, high = tile(t), tile(t, LANES)
            dest, upper, lower = (GM, -im, im) if left else (KM, im, -im)
            dest[low, LOW] = re
            dest[low, HIGH] = upper
            dest[high, LOW] = lower
            dest[high, HIGH] = re
        return carry

    with scope('build'):
        lax.fori_loop(0, TILES, build, 0)

    shifts = [[QUBITS - 1 - cz_ref[side, k] for side in range(2)] for k in range(QUBITS // 2)]

    def build_signs(t, carry):
        flat = (me * DEVICES * ROWS + sub + SUB * t) * LANES + lane
        parity = jnp.zeros_like(flat)
        for shift_a, shift_b in shifts:
            parity = parity ^ ((flat >> shift_a) & (flat >> shift_b))
        SG[tile(t), :] = plus_minus(parity & 1).astype(F32)
        return carry

    with scope('signs'):
        lax.fori_loop(0, DEVICES * TILES, build_signs, 0, unroll=4)

    def strided(ref, at):
        return [ref[pl.ds(at + part, SUB, stride=2), :] for part in range(2)]

    zero_tile = jnp.zeros((SUB, LANES), F32)
    zero_pair = (zero_tile, zero_tile)

    def raw_sums(t, carry):
        total, sums = carry
        value = [strided(X, pl.multiple_of(block * CHUNK + 2 * SUB * t, 2 * SUB)) for block in range(DEVICES)]
        dens = [norm(v) for v in value]
        done = []
        for (diff, cross), bit in zip(sums, (4, 2, 1)):
            for block in range(DEVICES):
                if block & bit:
                    diff = diff - dens[block]
                else:
                    diff = diff + dens[block]
                    cross = cadd(cross, conj_mul(value[block], value[block + bit]))
            done.append((diff, cross))
        for part in dens:
            total = total + part
        return total, tuple(done)

    with scope('raw'):
        raw_total, raw = lax.fori_loop(0, TILES, raw_sums, (zero_tile, ((zero_tile, zero_pair),) * 3))

    def fold(part):
        return jnp.sum(part, axis=0, keepdims=True)

    def pair_weights(mat):
        u00, u01, u10, u11 = mat
        (a_re, a_im), (b_re, b_im) = conj_mul(u00, u01), conj_mul(u10, u11)
        return norm(u00) - norm(u10), norm(u01) - norm(u11), 2 * (a_re - b_re), 2 * (b_im - a_im)

    raw_rows = []
    raw_total = fold(raw_total)
    for qubit, (diff, (re, im)) in zip((3, 4, 5), raw):
        weight_0, weight_1, mix_re, mix_im = pair_weights(matrix(qubit))
        even, odd = raw_total + fold(diff), raw_total - fold(diff)
        raw_rows.append((weight_0 * even + weight_1 * odd) / 2 + mix_re * fold(re) + mix_im * fold(im))

    def gate_pair(qubit, own_bit):
        return entry(qubit, own_bit, own_bit), entry(qubit, own_bit, 1 - own_bit)

    coef_y = gate_pair(0, bit_y)
    coef_x = gate_pair(1, bit_x)
    coef_c = gate_pair(2, bit_c)
    stage1_coefs = [[cmul(top, core) for core in coef_c for top in coef] for coef in (coef_x, coef_y)]

    norms = zero_pair
    for k in range(CHUNKS):
        with scope('w_s1'):
            wait_bytes(RB.at[0:2 * CHUNK], s1r.at[k])
        for half in range(2):
            forward(half, k).start()
        if k:
            for half in range(2):
                stage2(half, k - 1).start()
        if k == 0:
            wait_bytes(XP, cpr)
        with scope('w_fw'):
            wait_bytes(RP.at[0:2 * CHUNK], fwr.at[k])

        for half in range(2):
            coefs = stage1_coefs[half]
            base = (half * CHUNKS + sent(half, k)) * CHUNK

            def combine(t, carry, base=base, coefs=coefs, half=half):
                at = pl.multiple_of(base + 2 * SUB * t, 2 * SUB)
                re, im = mix(coefs, [strided(ref, at) for ref in (X, RB, XP, RP)])
                XC[tile(t), (LOW, HIGH)[half]] = re
                XC[tile(t, LANES), (LOW, HIGH)[half]] = im
                return carry

            with scope('comb'):
                lax.fori_loop(0, TILES, combine, 0, unroll=2)
        with scope('mm'):
            left = lax.dot(GM[...], XC[...], precision=lax.Precision.HIGHEST, preferred_element_type=F32)
            for rows in (LOW, HIGH):
                for cols in (LOW, HIGH):
                    ZC[cols, rows] = left[rows, cols]
            both = lax.dot(ZC[...], KM[...], precision=lax.Precision.HIGHEST, preferred_element_type=F32)
            for half in range(2):
                for part in range(2):
                    S[half, sent(half, k), part] = both[(LOW, HIGH)[half], (LOW, HIGH)[part]]

        def mid_sums(t, sums, k=k):
            dens = [norm(planes(S, half, sent(half, k), tile(t))) for half in range(2)]
            row = dens[0] + dens[1]
            TP[tile(t), :] = row if k == 0 else TP[tile(t), :] + row
            return tuple(a + b for a, b in zip(sums, dens))

        with scope('dens'):
            norms = lax.fori_loop(0, TILES, mid_sums, norms, unroll=2)

    flips = (1 - bit_y, 1 - bit_x)
    u3 = matrix(3)
    u4 = [matrix(4, flip) for flip in flips]
    u5 = [matrix(5, flip) for flip in flips]
    second_coef = (coef_y, coef_x)

    def second_gate(half, k, rows):
        chunk = received(half, k)
        return mix(second_coef[half], (planes(S, half, chunk, rows), planes(R2, half, chunk, rows)))

    def add_cross(k):
        def body(t, cross):
            done = []
            for half in range(2):
                chunk = received(half, k)
                part = conj_mul(planes(S, half, chunk, tile(t)), planes(R2, half, chunk, tile(t)))
                done.append(cadd(cross[half], part))
            return tuple(done)
        return body

    def step_even(k):
        def body(t, carry):
            for half in range(2):
                put(T, half, k, tile(t), second_gate(half, k, tile(t)))
            return carry
        return body

    def step_second(t, carry):
        rows = tile(t)
        for half in range(2):
            pair = gate(u5[half], planes(T, half, 0, rows), second_gate(half, 1, rows))
            for k, value in enumerate(pair):
                put(T, half, k, rows, value)
        return carry

    def step_last(t, carry):
        rows = tile(t)
        for half in range(2):
            upper = gate(u5[half], planes(T, half, 2, rows), second_gate(half, 3, rows))
            pairs = [gate(u4[half], planes(T, half, k, rows), upper[k]) for k in range(2)]
            for k in range(CHUNKS):
                put(T, half, received(half, k), rows, pairs[k % 2][k // 2])
        return carry

    def step_out(t, carry):
        rows = tile(t)
        for chunk in range(CHUNKS):
            for half, done in enumerate(gate(u3, planes(T, 0, chunk, rows), planes(T, 1, chunk, rows))):
                block = half * CHUNKS + chunk
                sign = SG[tile(t, block * ROWS), :]
                at = pl.multiple_of(block * CHUNK + 2 * SUB * t, 2 * SUB)
                for part in range(2):
                    OUT[pl.ds(at + part, SUB, stride=2), :] = done[part] * sign
        return carry

    cross = (zero_pair, zero_pair)
    with scope('w_s2'):
        wait_bytes(R2.at[:, 0], s2r.at[0])
    for piece in range(EARLY):
        for half in range(2):
            stage2(half, 3, piece).start()
    with scope('st0'):
        cross = lax.fori_loop(0, TILES, add_cross(0), cross, unroll=2)
        lax.fori_loop(0, TILES, step_even(0), 0, unroll=2)
    with scope('w_s2'):
        wait_bytes(R2.at[:, 0], s2r.at[1])
    with scope('x1'):
        cross = lax.fori_loop(0, TILES, add_cross(1), cross, unroll=2)

    def signed(parts, bit):
        acc = parts[0]
        for index, part in enumerate(parts[1:], 1):
            acc = acc - part if (index >> bit) & 1 else acc + part
        return acc

    def z_copy(dist):
        dev = me + (dist // 4) * step_y + (dist // 2 % 2) * step_x + (dist % 2) * step_c
        return remote(V, VR.at[dist], zs, zr, dev)

    row_index = lax.broadcasted_iota(jnp.int32, (3 * SUB, LANES), 0)
    col_index = lax.broadcasted_iota(jnp.int32, (3 * SUB, LANES), 1)
    with scope('zsum'):
        signs = [plus_minus(bit).astype(F32) for bit in (bit_y, bit_x, bit_c)]
        norm_rows = [fold(part) for part in norms]
        tot_row = norm_rows[0] + norm_rows[1]
        rows = []
        for half, bit in enumerate(second_bit):
            weight_0, weight_1, mix_re, mix_im = pair_weights(matrix(half))
            re, im = cross[half]
            rows.append(jnp.where(bit == 1, weight_1, weight_0) * norm_rows[half] + mix_re * fold(re)
                        + (mix_im * signs[half]) * fold(im) + signs[half] * norm_rows[1 - half])
        rows += [signs[2] * tot_row] + raw_rows
        parts = [TP[tile(t), :] for t in range(TILES)]
        rows += [fold(signed(parts, bit)) for bit in reversed(range(4))]
        total = norms[0] + norms[1]
        rows += [fold(total * plus_minus((sub >> bit) & 1).astype(F32)) for bit in reversed(range(3))]
        rows += [tot_row * plus_minus((lane[:1] >> bit) & 1).astype(F32) for bit in reversed(range(7))]
        rows += [jnp.zeros_like(tot_row)] * 4
        column = jnp.sum(jnp.concatenate(rows, axis=0), axis=1, keepdims=True)
        mine = jnp.sum(jnp.where(row_index == col_index, column, 0.0), axis=0, keepdims=True)
        V[...] = mine
    with scope('st1'):
        lax.fori_loop(0, TILES, step_second, 0, unroll=2)
    for dist in reversed(range(1, DEVICES)):
        z_copy(dist).start()
    for piece in range(EARLY, len(PIECES) - 1):
        for half in range(2):
            stage2(half, 3, piece).start()
    with scope('w_s2'):
        wait_bytes(R2.at[:, 0], s2r.at[2])
    with scope('st2'):
        lax.fori_loop(0, TILES, step_even(2), 0, unroll=2)

    for piece in range(len(PIECES) - 1):
        low, high = PIECES[piece], PIECES[piece + 1]
        with scope('w_s2'):
            wait_bytes(R2.at[:, 0, :, low:high], s2r.at[3 + piece])
        with scope('tail'):
            lax.fori_loop(low // SUB, high // SUB, step_last, 0)
            lax.fori_loop(low // SUB, high // SUB, step_out, 0)
        if piece == len(PIECES) - 3:
            with scope('w_z'):
                wait_bytes(VR.at[1:DEVICES], zr)
            acc = mine
            for dist in range(1, DEVICES):
                acc = acc + VR[dist]
            z_ref[...] = acc[:, :QUBITS] / 2 ** QUBITS

    with scope('w_send'):
        wait_bytes(X, s1s)
        wait_bytes(X, cps)
        wait_bytes(X, fws)
        wait_bytes(S, s2s)
        wait_bytes(VR.at[1:DEVICES], zs)


def writer(state_ref, z_ref, state_out, z_out, sems):
    copies = [pltpu.make_async_copy(state_ref, state_out, sems.at[0]), pltpu.make_async_copy(z_ref, z_out, sems.at[1])]
    for copy in copies:
        copy.start()
    for copy in copies:
        copy.wait()


def solution(mesh):
    def local_layer(state_local, unitaries, cz_pairs):
        size = state_local.shape[1]
        rows = 2 * size // LANES
        x = state_local.reshape(2, -1, LANES).swapaxes(0, 1).reshape(rows, LANES)
        u = unitaries.transpose(0, 2, 3, 1).reshape(SUB, QUBITS)
        cz = cz_pairs.T
        x, u, cz = [pltpu.with_memory_space_constraint(v, pltpu.HBM) for v in (x, u, cz)]
        vm = pltpu.VMEM
        dma = pltpu.SemaphoreType.DMA
        full = vm((rows, LANES), F32)
        halves = vm((2, CHUNKS, 2, ROWS, LANES), F32)
        square = vm((2 * LANES, 2 * LANES), F32)
        any_spec = pl.BlockSpec(memory_space=pl.ANY)
        shapes = (jax.ShapeDtypeStruct((rows, LANES), F32), jax.ShapeDtypeStruct((1, QUBITS), F32))
        out, z = pl.pallas_call(
            kernel,
            out_shape=shapes,
            in_specs=[pl.BlockSpec(memory_space=pltpu.HBM)] * 3,
            out_specs=(pl.BlockSpec(memory_space=pltpu.VMEM), pl.BlockSpec(memory_space=pltpu.VMEM)),
            scratch_shapes=[
                full, pltpu.SMEM(u.shape, F32), pltpu.SMEM(cz.shape, jnp.int32), full, full, full, halves, halves, halves,
                vm((rows // 2, LANES), F32), square, square, square, square, vm((ROWS, LANES), F32),
                vm((1, LANES), F32), vm((DEVICES, 1, LANES), F32),
                dma((4,)), dma, dma((4,)), dma, dma, dma, dma((4,)), dma, dma((3 + len(PIECES) - 1,)), dma, dma,
            ],
            compiler_params=pltpu.CompilerParams(collective_id=0, has_side_effects=True, vmem_limit_bytes=40 * 2 ** 20),
        )(x, u, cz)
        out, z = pl.pallas_call(
            writer, out_shape=shapes, in_specs=[any_spec] * 2, out_specs=(any_spec,) * 2, scratch_shapes=[dma((2,))],
            compiler_params=pltpu.CompilerParams(vmem_limit_bytes=2 ** 20),
        )(out, z)
        state = out.reshape(-1, 2, LANES).swapaxes(0, 1).reshape(2, size)
        return state, z.reshape(QUBITS)

    return jax.shard_map(local_layer, mesh=mesh, in_specs=(P(None, 'q'), P(), P()), out_specs=(P(None, 'q'), P()), check_vma=False)
```

time: 195 us -> 30.2 us (0.15)
  the two profiles are of different devices: /device:TPU:1 before, /device:TPU:0 now
where the time goes in v2:
time: 30.2 us; the launch traced here: 30.1 us
  Pallas kernels  29.4 us (97%)
  between operations  0.64 us (2%)
    pallas_call x1, Pallas kernels, local_layer(): pl.pallas_call(kernel, out_shape=shapes, in_specs=[pl.BlockSpec(memory_sp...  28.5 us
    pallas_call x1, Pallas kernels, local_layer(): pl.pallas_call(writer, out_shape=shapes, in_specs=[any_spec] * 2, out_spe...  0.99 us

profile of v2, /device:TPU:0, one launch (start us, length us, event | category | flops | bytes accessed | tf_op | source)
XLA Modules:
  0.0 30.1 jit_solution(4804278380055657026)
XLA Ops:
  0.6 28.5 %shard_map.50 = (f32[2048,128]{1,0:T(8,128)S(1)}, f32[1,20]{1,0:T(1,128)S(1)}) custom-call(f32[2048,128]{1,0:T(8,128)} %bitcast.15, f32[8,20]{1,0:T(8,128)} %bitcast.16, s32[2,10]{1,0:T(2,128)} %bitcast.17), custom_call_target="tpu_custom_call" | custom-call | tf_op jit(solution)/shard_map/pallas_call | solution.py:460
  29.1 1.0 %shard_map.51 = (f32[2048,128]{1,0:T(8,128)}, f32[1,20]{1,0:T(1,128)}) custom-call(f32[2048,128]{1,0:T(8,128)S(1)} %get-tuple-element.6.state_ref, f32[1,20]{1,0:T(1,128)S(1)} %get-tuple-element.7.z_ref), custom_call_target="tpu_custom_call" | custom-call | tf_op jit(solution)/shard_map/pallas_call | solution.py:473

commit v3 on v2

--- a/solution.py
+++ b/solution.py
@@ -14,8 +14,9 @@
 ROWS = SUB * TILES
 CHUNK = 2 * ROWS
 CHUNKS = 4
-PIECES = (0, 48, 88, 112, 128)
-EARLY = 2
+PIECES = (0, 24, 72, 112, 128)
+FIRST = CHUNK // 4
+EARLY = 1
 DEVICES = 8
 QUBITS = 20
 scope = jax.named_scope
@@ -72,8 +73,9 @@
 
 
 def kernel(x_hbm, u_hbm, cz_hbm, OUT, z_ref,
-           X, u_ref, cz_ref, RB, XP, RP, S, R2, T, SG, GM, KM, XC, ZC, TP, V, VR,
-           ld, s1s, s1r, cps, cpr, fws, fwr, s2s, s2r, zs, zr):
+           BIG, u_ref, cz_ref, S, R2, T, SG, GM, KM, XC, ZC, TP, V, VR,
+           ld, sent_sem, s1r, cpr, fwr, s2r, zs, zr):
+    X, RB, XP, RP = [BIG.at[part] for part in range(4)]
     me = lax.axis_index('q')
     bit_y = me // 4
     bit_x = (me // 2) % 2
@@ -100,34 +102,39 @@
     def wait_bytes(ref, sem):
         pltpu.make_async_copy(ref, ref, sem).wait()
 
-    def load_copy(half, k):
-        rows = block_rows(half, sent(half, k))
-        return pltpu.make_async_copy(x_hbm.at[rows], X.at[rows], ld.at[min(k, 1)])
-
-    def stage1(half, k):
-        rows = block_rows(half, sent(half, k))
-        return remote(X.at[rows], RB.at[rows], s1s, s1r.at[k], first_dev[half])
+    def part_rows(half, k, part):
+        low, size = ((0, FIRST), (FIRST, CHUNK - FIRST))[part] if k == 0 else (0, CHUNK)
+        return pl.ds(pl.multiple_of((half * CHUNKS + sent(half, k)) * CHUNK + low, SUB), size)
+
+    def load_copy(half, k, part=0):
+        rows = part_rows(half, k, part)
+        return pltpu.make_async_copy(x_hbm.at[rows], X.at[rows], ld.at[min(2, k + 1) if k else part])
+
+    def stage1(half, k, part=0):
+        rows = part_rows(half, k, part)
+        return remote(X.at[rows], RB.at[rows], sent_sem, s1r.at[k], first_dev[half])
 
     def core_copy(half, k):
         rows = block_rows(half, sent(half, k))
-        return remote(X.at[rows], XP.at[rows], cps, cpr, dev_c)
+        return remote(X.at[rows], XP.at[rows], sent_sem, cpr, dev_c)
 
     def forward(half, k):
         rows = block_rows(half, sent(half, k))
-        return remote(RB.at[rows], RP.at[rows], fws, fwr.at[k], dev_c)
+        return remote(RB.at[rows], RP.at[rows], sent_sem, fwr.at[k], dev_c)
 
     def stage2(half, k, piece=None):
         chunk = sent(half, k)
         if piece is None:
-            return remote(S.at[half, chunk], R2.at[half, chunk], s2s, s2r.at[k], second_dev[half])
+            return remote(S.at[half, chunk], R2.at[half, chunk], sent_sem, s2r.at[k], second_dev[half])
         rows = pl.ds(PIECES[piece], PIECES[piece + 1] - PIECES[piece])
-        return remote(S.at[half, chunk, :, rows], R2.at[half, chunk, :, rows], s2s, s2r.at[3 + piece], second_dev[half])
-
-    u_copy = pltpu.make_async_copy(u_hbm, u_ref, ld.at[2])
-    cz_copy = pltpu.make_async_copy(cz_hbm, cz_ref, ld.at[3])
-    for k in range(CHUNKS):
-        for half in range(2):
-            load_copy(half, k).start()
+        return remote(S.at[half, chunk, :, rows], R2.at[half, chunk, :, rows], sent_sem, s2r.at[3 + piece], second_dev[half])
+
+    u_copy = pltpu.make_async_copy(u_hbm, u_ref, ld.at[3])
+    cz_copy = pltpu.make_async_copy(cz_hbm, cz_ref, ld.at[4])
+    order = [(k, part) for k in range(CHUNKS) for part in range(1 if k else 2)]
+    for k, part in order:
+        for half in range(2):
+            load_copy(half, k, part).start()
     u_copy.start()
     cz_copy.start()
 
@@ -137,15 +144,14 @@
     with scope('bar'):
         pl.semaphore_wait(barrier, 3)
 
-    with scope('w_ld'):
-        wait_bytes(X.at[0:2 * CHUNK], ld.at[0])
-    for half in range(2):
-        stage1(half, 0).start()
-    with scope('w_ld'):
-        wait_bytes(X.at[0:6 * CHUNK], ld.at[1])
-    for k in range(1, CHUNKS):
-        for half in range(2):
-            stage1(half, k).start()
+    waits = {(0, 0): (0, 2 * FIRST), (0, 1): (1, 2 * (CHUNK - FIRST)), (1, 0): (2, 6 * CHUNK)}
+    for k, part in order:
+        if (k, part) in waits:
+            index, size = waits[k, part]
+            with scope('w_ld'):
+                wait_bytes(X.at[:size], ld.at[index])
+        for half in range(2):
+            stage1(half, k, part).start()
     for k in range(CHUNKS):
         for half in range(2):
             core_copy(half, k).start()
@@ -304,9 +310,16 @@
     u5 = [matrix(5, flip) for flip in flips]
     second_coef = (coef_y, coef_x)
 
-    def second_gate(half, k, rows):
-        chunk = received(half, k)
-        return mix(second_coef[half], (planes(S, half, chunk, rows), planes(R2, half, chunk, rows)))
+    def weights(k):
+        table = {}
+        for half in range(2):
+            index = received(half, k)
+            for chunk in range(CHUNKS):
+                inner = cmul(entry(4, chunk // 2, index // 2), entry(5, chunk % 2, index % 2))
+                inner = cmul(second_coef[half][1], inner)
+                for side in range(2):
+                    table[side, chunk, half] = cmul(u3[2 * side + half], inner)
+        return table
 
     def add_cross(k):
         def body(t, cross):
@@ -318,50 +331,60 @@
             return tuple(done)
         return body
 
-    def step_even(k):
+    def step_own(t, carry):
+        rows = tile(t)
+        for half in range(2):
+            own, other = second_coef[half]
+            value = []
+            for k in range(CHUNKS):
+                chunk = received(half, k)
+                part = cmul(own, planes(S, half, chunk, rows))
+                value.append(cadd(part, cmul(other, planes(R2, half, chunk, rows))) if k < 2 else part)
+            value = [v for pair in (value[:2], value[2:]) for v in gate(u5[half], *pair)]
+            value = [gate(u4[half], value[k], value[k + 2]) for k in range(2)]
+            for k in range(CHUNKS):
+                put(T, half, received(half, k), rows, value[k % 2][k // 2])
+        return carry
+
+    def step_mix(t, carry):
+        rows = tile(t)
+        for chunk in range(CHUNKS):
+            for half, value in enumerate(gate(u3, planes(T, 0, chunk, rows), planes(T, 1, chunk, rows))):
+                put(T, half, chunk, rows, value)
+        return carry
+
+    def add_received(k, table, store):
         def body(t, carry):
-            for half in range(2):
-                put(T, half, k, tile(t), second_gate(half, k, tile(t)))
+            rows = tile(t)
+            other = [planes(R2, half, received(half, k), rows) for half in range(2)]
+            for side in range(2):
+                for chunk in range(CHUNKS):
+                    value = planes(T, side, chunk, rows)
+                    for half in range(2):
+                        value = cadd(value, cmul(table[side, chunk, half], other[half]))
+                    store(side, chunk, t, value)
             return carry
         return body
 
-    def step_second(t, carry):
-        rows = tile(t)
-        for half in range(2):
-            pair = gate(u5[half], planes(T, half, 0, rows), second_gate(half, 1, rows))
-            for k, value in enumerate(pair):
-                put(T, half, k, rows, value)
-        return carry
-
-    def step_last(t, carry):
-        rows = tile(t)
-        for half in range(2):
-            upper = gate(u5[half], planes(T, half, 2, rows), second_gate(half, 3, rows))
-            pairs = [gate(u4[half], planes(T, half, k, rows), upper[k]) for k in range(2)]
-            for k in range(CHUNKS):
-                put(T, half, received(half, k), rows, pairs[k % 2][k // 2])
-        return carry
-
-    def step_out(t, carry):
-        rows = tile(t)
-        for chunk in range(CHUNKS):
-            for half, done in enumerate(gate(u3, planes(T, 0, chunk, rows), planes(T, 1, chunk, rows))):
-                block = half * CHUNKS + chunk
-                sign = SG[tile(t, block * ROWS), :]
-                at = pl.multiple_of(block * CHUNK + 2 * SUB * t, 2 * SUB)
-                for part in range(2):
-                    OUT[pl.ds(at + part, SUB, stride=2), :] = done[part] * sign
-        return carry
-
+    def store_partial(side, chunk, t, value):
+        put(T, side, chunk, tile(t), value)
+
+    def store_out(side, chunk, t, value):
+        block = side * CHUNKS + chunk
+        sign = SG[tile(t, block * ROWS), :]
+        at = pl.multiple_of(block * CHUNK + 2 * SUB * t, 2 * SUB)
+        for part in range(2):
+            OUT[pl.ds(at + part, SUB, stride=2), :] = value[part] * sign
+
+    tables = {k: weights(k) for k in (2, 3)}
     cross = (zero_pair, zero_pair)
     with scope('w_s2'):
         wait_bytes(R2.at[:, 0], s2r.at[0])
     for piece in range(EARLY):
         for half in range(2):
             stage2(half, 3, piece).start()
-    with scope('st0'):
+    with scope('x0'):
         cross = lax.fori_loop(0, TILES, add_cross(0), cross, unroll=2)
-        lax.fori_loop(0, TILES, step_even(0), 0, unroll=2)
     with scope('w_s2'):
         wait_bytes(R2.at[:, 0], s2r.at[1])
     with scope('x1'):
@@ -399,25 +422,25 @@
         column = jnp.sum(jnp.concatenate(rows, axis=0), axis=1, keepdims=True)
         mine = jnp.sum(jnp.where(row_index == col_index, column, 0.0), axis=0, keepdims=True)
         V[...] = mine
-    with scope('st1'):
-        lax.fori_loop(0, TILES, step_second, 0, unroll=2)
     for dist in reversed(range(1, DEVICES)):
         z_copy(dist).start()
     for piece in range(EARLY, len(PIECES) - 1):
         for half in range(2):
             stage2(half, 3, piece).start()
+    with scope('own'):
+        lax.fori_loop(0, TILES, step_own, 0)
+        lax.fori_loop(0, TILES, step_mix, 0)
     with scope('w_s2'):
         wait_bytes(R2.at[:, 0], s2r.at[2])
     with scope('st2'):
-        lax.fori_loop(0, TILES, step_even(2), 0, unroll=2)
+        lax.fori_loop(0, TILES, add_received(2, tables[2], store_partial), 0)
 
     for piece in range(len(PIECES) - 1):
         low, high = PIECES[piece], PIECES[piece + 1]
         with scope('w_s2'):
             wait_bytes(R2.at[:, 0, :, low:high], s2r.at[3 + piece])
         with scope('tail'):
-            lax.fori_loop(low // SUB, high // SUB, step_last, 0)
-            lax.fori_loop(low // SUB, high // SUB, step_out, 0)
+            lax.fori_loop(low // SUB, high // SUB, add_received(3, tables[3], store_out), 0)
         if piece == len(PIECES) - 3:
             with scope('w_z'):
                 wait_bytes(VR.at[1:DEVICES], zr)
@@ -427,10 +450,7 @@
             z_ref[...] = acc[:, :QUBITS] / 2 ** QUBITS
 
     with scope('w_send'):
-        wait_bytes(X, s1s)
-        wait_bytes(X, cps)
-        wait_bytes(X, fws)
-        wait_bytes(S, s2s)
+        wait_bytes(BIG, sent_sem)
         wait_bytes(VR.at[1:DEVICES], zs)
 
 
@@ -452,7 +472,6 @@
         x, u, cz = [pltpu.with_memory_space_constraint(v, pltpu.HBM) for v in (x, u, cz)]
         vm = pltpu.VMEM
         dma = pltpu.SemaphoreType.DMA
-        full = vm((rows, LANES), F32)
         halves = vm((2, CHUNKS, 2, ROWS, LANES), F32)
         square = vm((2 * LANES, 2 * LANES), F32)
         any_spec = pl.BlockSpec(memory_space=pl.ANY)
@@ -463,10 +482,10 @@
             in_specs=[pl.BlockSpec(memory_space=pltpu.HBM)] * 3,
             out_specs=(pl.BlockSpec(memory_space=pltpu.VMEM), pl.BlockSpec(memory_space=pltpu.VMEM)),
             scratch_shapes=[
-                full, pltpu.SMEM(u.shape, F32), pltpu.SMEM(cz.shape, jnp.int32), full, full, full, halves, halves, halves,
+                vm((4, rows, LANES), F32), pltpu.SMEM(u.shape, F32), pltpu.SMEM(cz.shape, jnp.int32), halves, halves, halves,
                 vm((rows // 2, LANES), F32), square, square, square, square, vm((ROWS, LANES), F32),
                 vm((1, LANES), F32), vm((DEVICES, 1, LANES), F32),
-                dma((4,)), dma, dma((4,)), dma, dma, dma, dma((4,)), dma, dma((3 + len(PIECES) - 1,)), dma, dma,
+                dma((5,)), dma, dma((4,)), dma, dma((4,)), dma((3 + len(PIECES) - 1,)), dma, dma,
             ],
             compiler_params=pltpu.CompilerParams(collective_id=0, has_side_effects=True, vmem_limit_bytes=40 * 2 ** 20),
         )(x, u, cz)

time: 30.2 us -> 29.9 us (0.990)
  no operation moved by 1% of the time
where the time goes in v3:
time: 29.9 us; the launch traced here: 29.8 us
  Pallas kernels  29.2 us (98%)
  between operations  0.64 us (2%)
    pallas_call x1, Pallas kernels, local_layer(): pl.pallas_call(kernel, out_shape=shapes, in_specs=[pl.BlockSpec(memory_sp...  28.2 us
    pallas_call x1, Pallas kernels, local_layer(): pl.pallas_call(writer, out_shape=shapes, in_specs=[any_spec] * 2, out_spe...  0.99 us

profile of v3, /device:TPU:0, one launch (start us, length us, event | category | flops | bytes accessed | tf_op | source)
XLA Modules:
  0.0 29.8 jit_solution(17658805426349372420)
XLA Ops:
  0.6 28.2 %shard_map.50 = (f32[2048,128]{1,0:T(8,128)S(1)}, f32[1,20]{1,0:T(1,128)S(1)}) custom-call(f32[2048,128]{1,0:T(8,128)} %bitcast.15, f32[8,20]{1,0:T(8,128)} %bitcast.16, s32[2,10]{1,0:T(2,128)} %bitcast.17), custom_call_target="tpu_custom_call" | custom-call | tf_op jit(solution)/shard_map/pallas_call | solution.py:479
  28.8 1.0 %shard_map.51 = (f32[2048,128]{1,0:T(8,128)}, f32[1,20]{1,0:T(1,128)}) custom-call(f32[2048,128]{1,0:T(8,128)S(1)} %get-tuple-element.6.state_ref, f32[1,20]{1,0:T(1,128)S(1)} %get-tuple-element.7.z_ref), custom_call_target="tpu_custom_call" | custom-call | tf_op jit(solution)/shard_map/pallas_call | solution.py:492

commit v4 on v3

--- a/solution.py
+++ b/solution.py
@@ -14,9 +14,10 @@
 ROWS = SUB * TILES
 CHUNK = 2 * ROWS
 CHUNKS = 4
-PIECES = (0, 24, 72, 112, 128)
+PIECES = (0, 24, 40, 72, 104, 128)
 FIRST = CHUNK // 4
 EARLY = 1
+HELD = 2
 DEVICES = 8
 QUBITS = 20
 scope = jax.named_scope
@@ -131,6 +132,9 @@
 
     u_copy = pltpu.make_async_copy(u_hbm, u_ref, ld.at[3])
     cz_copy = pltpu.make_async_copy(cz_hbm, cz_ref, ld.at[4])
+    barrier = pltpu.get_barrier_semaphore()
+    for dev in (dev_x, dev_y, dev_c):
+        pl.semaphore_signal(barrier, inc=1, device_id=(dev,), device_id_type=MESH)
     order = [(k, part) for k in range(CHUNKS) for part in range(1 if k else 2)]
     for k, part in order:
         for half in range(2):
@@ -138,9 +142,6 @@
     u_copy.start()
     cz_copy.start()
 
-    barrier = pltpu.get_barrier_semaphore()
-    for dev in (dev_x, dev_y, dev_c):
-        pl.semaphore_signal(barrier, inc=1, device_id=(dev,), device_id_type=MESH)
     with scope('bar'):
         pl.semaphore_wait(barrier, 3)
 
@@ -424,9 +425,13 @@
         V[...] = mine
     for dist in reversed(range(1, DEVICES)):
         z_copy(dist).start()
-    for piece in range(EARLY, len(PIECES) - 1):
-        for half in range(2):
-            stage2(half, 3, piece).start()
+    def send_pieces(low, high):
+        for piece in range(low, high):
+            for half in range(2):
+                stage2(half, 3, piece).start()
+
+    send_pieces(EARLY, HELD)
+    pl.when(bit_c == 0)(lambda: send_pieces(HELD, len(PIECES) - 1))
     with scope('own'):
         lax.fori_loop(0, TILES, step_own, 0)
         lax.fori_loop(0, TILES, step_mix, 0)
@@ -439,6 +444,8 @@
         low, high = PIECES[piece], PIECES[piece + 1]
         with scope('w_s2'):
             wait_bytes(R2.at[:, 0, :, low:high], s2r.at[3 + piece])
+        if piece == 1:
+            pl.when(bit_c == 1)(lambda: send_pieces(HELD, len(PIECES) - 1))
         with scope('tail'):
             lax.fori_loop(low // SUB, high // SUB, add_received(3, tables[3], store_out), 0)
         if piece == len(PIECES) - 3:

time: 29.9 us -> 29.1 us (0.973)
  the two profiles are of different devices: /device:TPU:0 before, /device:TPU:1 now
where the time goes in v4:
time: 29.1 us; the launch traced here: 29 us
  Pallas kernels  28.3 us (97%)
  between operations  0.64 us (2%)
    pallas_call x1, Pallas kernels, local_layer(): pl.pallas_call(kernel, out_shape=shapes, in_specs=[pl.BlockSpec(memory_sp...  27.3 us
    pallas_call x1, Pallas kernels, local_layer(): pl.pallas_call(writer, out_shape=shapes, in_specs=[any_spec] * 2, out_spe...  0.99 us

profile of v4, /device:TPU:1, one launch (start us, length us, event | category | flops | bytes accessed | tf_op | source)
XLA Modules:
  0.0 29.0 jit_solution(1078904765088248246)
XLA Ops:
  0.6 27.3 %shard_map.50 = (f32[2048,128]{1,0:T(8,128)S(1)}, f32[1,20]{1,0:T(1,128)S(1)}) custom-call(f32[2048,128]{1,0:T(8,128)} %bitcast.15, f32[8,20]{1,0:T(8,128)} %bitcast.16, s32[2,10]{1,0:T(2,128)} %bitcast.17), custom_call_target="tpu_custom_call" | custom-call | tf_op jit(solution)/shard_map/pallas_call | solution.py:486
  28.0 1.0 %shard_map.51 = (f32[2048,128]{1,0:T(8,128)}, f32[1,20]{1,0:T(1,128)}) custom-call(f32[2048,128]{1,0:T(8,128)S(1)} %get-tuple-element.6.state_ref, f32[1,20]{1,0:T(1,128)S(1)} %get-tuple-element.7.z_ref), custom_call_target="tpu_custom_call" | custom-call | tf_op jit(solution)/shard_map/pallas_call | solution.py:499

commit v5 on v4

--- a/solution.py
+++ b/solution.py
@@ -17,7 +17,6 @@
 PIECES = (0, 24, 40, 72, 104, 128)
 FIRST = CHUNK // 4
 EARLY = 1
-HELD = 2
 DEVICES = 8
 QUBITS = 20
 scope = jax.named_scope
@@ -75,7 +74,7 @@
 
 def kernel(x_hbm, u_hbm, cz_hbm, OUT, z_ref,
            BIG, u_ref, cz_ref, S, R2, T, SG, GM, KM, XC, ZC, TP, V, VR,
-           ld, sent_sem, s1r, cpr, fwr, s2r, zs, zr):
+           ld, sent_sem, s1r, cpr, fwr, s2r, zs, zr, ready):
     X, RB, XP, RP = [BIG.at[part] for part in range(4)]
     me = lax.axis_index('q')
     bit_y = me // 4
@@ -132,9 +131,16 @@
 
     u_copy = pltpu.make_async_copy(u_hbm, u_ref, ld.at[3])
     cz_copy = pltpu.make_async_copy(cz_hbm, cz_ref, ld.at[4])
+    last_chip = bit_y * bit_x
+    beside = bit_y + bit_x - 2 * last_chip
     barrier = pltpu.get_barrier_semaphore()
-    for dev in (dev_x, dev_y, dev_c):
-        pl.semaphore_signal(barrier, inc=1, device_id=(dev,), device_id_type=MESH)
+
+    def signal(sem, devices):
+        for dev in devices:
+            pl.semaphore_signal(sem, inc=1, device_id=(dev,), device_id_type=MESH)
+
+    signal(barrier, (dev_c,))
+    pl.when(last_chip == 0)(lambda: signal(barrier, (dev_x, dev_y)))
     order = [(k, part) for k in range(CHUNKS) for part in range(1 if k else 2)]
     for k, part in order:
         for half in range(2):
@@ -142,17 +148,37 @@
     u_copy.start()
     cz_copy.start()
 
+    waits = {(0, 0): (0, 2 * FIRST), (0, 1): (1, 2 * (CHUNK - FIRST)), (1, 0): (2, 6 * CHUNK)}
+
+    def send_first(halves, wait):
+        for k, part in order:
+            if wait and (k, part) in waits:
+                index, size = waits[k, part]
+                wait_bytes(X.at[:size], ld.at[index])
+            if k == 0:
+                for half in halves:
+                    stage1(half, k, part).start()
+        pl.when(bit_c == 0)(lambda: send_rest(halves))
+
+    def send_rest(halves):
+        for k in range(1, CHUNKS):
+            for half in halves:
+                stage1(half, k).start()
+
+    def send_beside(half):
+        send_first((half,), True)
+        with scope('w_rdy'):
+            pl.semaphore_wait(ready, 1)
+        send_first((1 - half,), False)
+
     with scope('bar'):
-        pl.semaphore_wait(barrier, 3)
-
-    waits = {(0, 0): (0, 2 * FIRST), (0, 1): (1, 2 * (CHUNK - FIRST)), (1, 0): (2, 6 * CHUNK)}
-    for k, part in order:
-        if (k, part) in waits:
-            index, size = waits[k, part]
-            with scope('w_ld'):
-                wait_bytes(X.at[:size], ld.at[index])
-        for half in range(2):
-            stage1(half, k, part).start()
+        pl.when(beside == 1)(lambda: pl.semaphore_wait(barrier, 2))
+        pl.when(beside == 0)(lambda: pl.semaphore_wait(barrier, 3))
+    pl.when(last_chip == 1)(lambda: signal(ready, (dev_x, dev_y)))
+    with scope('first'):
+        pl.when(beside == 0)(lambda: send_first((0, 1), True))
+        pl.when(beside * bit_x == 1)(lambda: send_beside(0))
+        pl.when(beside * bit_y == 1)(lambda: send_beside(1))
     for k in range(CHUNKS):
         for half in range(2):
             core_copy(half, k).start()
@@ -265,7 +291,9 @@
             wait_bytes(RB.at[0:2 * CHUNK], s1r.at[k])
         for half in range(2):
             forward(half, k).start()
-        if k:
+        if k == 0:
+            pl.when(bit_c == 1)(lambda: send_rest((0, 1)))
+        else:
             for half in range(2):
                 stage2(half, k - 1).start()
         if k == 0:
@@ -430,8 +458,7 @@
             for half in range(2):
                 stage2(half, 3, piece).start()
 
-    send_pieces(EARLY, HELD)
-    pl.when(bit_c == 0)(lambda: send_pieces(HELD, len(PIECES) - 1))
+    send_pieces(EARLY, len(PIECES) - 1)
     with scope('own'):
         lax.fori_loop(0, TILES, step_own, 0)
         lax.fori_loop(0, TILES, step_mix, 0)
@@ -444,8 +471,6 @@
         low, high = PIECES[piece], PIECES[piece + 1]
         with scope('w_s2'):
             wait_bytes(R2.at[:, 0, :, low:high], s2r.at[3 + piece])
-        if piece == 1:
-            pl.when(bit_c == 1)(lambda: send_pieces(HELD, len(PIECES) - 1))
         with scope('tail'):
             lax.fori_loop(low // SUB, high // SUB, add_received(3, tables[3], store_out), 0)
         if piece == len(PIECES) - 3:
@@ -492,7 +517,7 @@
                 vm((4, rows, LANES), F32), pltpu.SMEM(u.shape, F32), pltpu.SMEM(cz.shape, jnp.int32), halves, halves, halves,
                 vm((rows // 2, LANES), F32), square, square, square, square, vm((ROWS, LANES), F32),
                 vm((1, LANES), F32), vm((DEVICES, 1, LANES), F32),
-                dma((5,)), dma, dma((4,)), dma, dma((4,)), dma((3 + len(PIECES) - 1,)), dma, dma,
+                dma((5,)), dma, dma((4,)), dma, dma((4,)), dma((3 + len(PIECES) - 1,)), dma, dma, pltpu.SemaphoreType.REGULAR,
             ],
             compiler_params=pltpu.CompilerParams(collective_id=0, has_side_effects=True, vmem_limit_bytes=40 * 2 ** 20),
         )(x, u, cz)

time: 29.1 us -> 28.5 us (0.979)
  Pallas kernels: 28.3 us -> 27.7 us
    pallas_call x1, Pallas kernels: 27.3 us -> 26.7 us  [local_layer(): pl.pallas_call(kernel, out_shape=shapes, in_specs=[pl.BlockSpec(memory_sp...]
where the time goes in v5:
time: 28.5 us; the launch traced here: 28.4 us
  Pallas kernels  27.7 us (97%)
  between operations  0.64 us (2%)
    pallas_call x1, Pallas kernels, local_layer(): pl.pallas_call(kernel, out_shape=shapes, in_specs=[pl.BlockSpec(memory_sp...  26.7 us
    pallas_call x1, Pallas kernels, local_layer(): pl.pallas_call(writer, out_shape=shapes, in_specs=[any_spec] * 2, out_spe...  0.99 us

profile of v5, /device:TPU:1, one launch (start us, length us, event | category | flops | bytes accessed | tf_op | source)
XLA Modules:
  0.0 28.4 jit_solution(3338464435965797670)
XLA Ops:
  0.6 26.7 %shard_map.50 = (f32[2048,128]{1,0:T(8,128)S(1)}, f32[1,20]{1,0:T(1,128)S(1)}) custom-call(f32[2048,128]{1,0:T(8,128)} %bitcast.15, f32[8,20]{1,0:T(8,128)} %bitcast.16, s32[2,10]{1,0:T(2,128)} %bitcast.17), custom_call_target="tpu_custom_call" | custom-call | tf_op jit(solution)/shard_map/pallas_call | solution.py:511
  27.4 1.0 %shard_map.51 = (f32[2048,128]{1,0:T(8,128)}, f32[1,20]{1,0:T(1,128)}) custom-call(f32[2048,128]{1,0:T(8,128)S(1)} %get-tuple-element.6.state_ref, f32[1,20]{1,0:T(1,128)S(1)} %get-tuple-element.7.z_ref), custom_call_target="tpu_custom_call" | custom-call | tf_op jit(solution)/shard_map/pallas_call | solution.py:524

commit v6 on v5

--- a/solution.py
+++ b/solution.py
@@ -14,10 +14,11 @@
 ROWS = SUB * TILES
 CHUNK = 2 * ROWS
 CHUNKS = 4
-PIECES = (0, 24, 40, 72, 104, 128)
+PIECES = (0, 16, 64, 112, 128)
 FIRST = CHUNK // 4
-EARLY = 1
+EARLY = 0
 DEVICES = 8
+CHIPS = 4
 QUBITS = 20
 scope = jax.named_scope
 
@@ -73,8 +74,8 @@
 
 
 def kernel(x_hbm, u_hbm, cz_hbm, OUT, z_ref,
-           BIG, u_ref, cz_ref, S, R2, T, SG, GM, KM, XC, ZC, TP, V, VR,
-           ld, sent_sem, s1r, cpr, fwr, s2r, zs, zr, ready):
+           BIG, u_ref, cz_ref, S, R2, T, SG, GM, KM, XC, ZC, TP, V, VP, VR, V7,
+           ld, sent_sem, s1r, cpr, fwr, s2r, zs, zr, zp, ready):
     X, RB, XP, RP = [BIG.at[part] for part in range(4)]
     me = lax.axis_index('q')
     bit_y = me // 4
@@ -425,9 +426,25 @@
             acc = acc - part if (index >> bit) & 1 else acc + part
         return acc
 
-    def z_copy(dist):
-        dev = me + (dist // 4) * step_y + (dist // 2 % 2) * step_x + (dist % 2) * step_c
-        return remote(V, VR.at[dist], zs, zr, dev)
+    def z_part():
+        return remote(V, VP, zs, zp, dev_c)
+
+    def z_copy(chip, core):
+        dev = me + (chip // 2) * step_y + (chip % 2) * step_x + core * step_c
+        return remote(V, VR.at[chip], zs, zr, dev)
+
+    def send_sum():
+        with scope('w_zp'):
+            wait_bytes(VP, zp)
+        total = V[...] + VP[...]
+        V[...] = total
+        VR[0] = total
+
+    def spread_sum():
+        for chip in reversed(range(CHIPS)):
+            for core in reversed(range(2)):
+                if chip or core:
+                    z_copy(chip, core).start()
 
     row_index = lax.broadcasted_iota(jnp.int32, (3 * SUB, LANES), 0)
     col_index = lax.broadcasted_iota(jnp.int32, (3 * SUB, LANES), 1)
@@ -451,8 +468,9 @@
         column = jnp.sum(jnp.concatenate(rows, axis=0), axis=1, keepdims=True)
         mine = jnp.sum(jnp.where(row_index == col_index, column, 0.0), axis=0, keepdims=True)
         V[...] = mine
-    for dist in reversed(range(1, DEVICES)):
-        z_copy(dist).start()
+    pl.when(bit_c == 1)(send_sum)
+    pl.when(bit_c == 0)(lambda: z_part().start())
+    pl.when(bit_c == 1)(spread_sum)
     def send_pieces(low, high):
         for piece in range(low, high):
             for half in range(2):
@@ -475,15 +493,17 @@
             lax.fori_loop(low // SUB, high // SUB, add_received(3, tables[3], store_out), 0)
         if piece == len(PIECES) - 3:
             with scope('w_z'):
-                wait_bytes(VR.at[1:DEVICES], zr)
-            acc = mine
-            for dist in range(1, DEVICES):
-                acc = acc + VR[dist]
+                pl.when(bit_c == 0)(lambda: wait_bytes(VR, zr))
+                pl.when(bit_c == 1)(lambda: wait_bytes(VR.at[1:CHIPS], zr))
+            acc = VR[0]
+            for chip in range(1, CHIPS):
+                acc = acc + VR[chip]
             z_ref[...] = acc[:, :QUBITS] / 2 ** QUBITS
 
     with scope('w_send'):
         wait_bytes(BIG, sent_sem)
-        wait_bytes(VR.at[1:DEVICES], zs)
+        pl.when(bit_c == 0)(lambda: wait_bytes(VP, zs))
+        pl.when(bit_c == 1)(lambda: wait_bytes(V7, zs))
 
 
 def writer(state_ref, z_ref, state_out, z_out, sems):
@@ -516,8 +536,8 @@
             scratch_shapes=[
                 vm((4, rows, LANES), F32), pltpu.SMEM(u.shape, F32), pltpu.SMEM(cz.shape, jnp.int32), halves, halves, halves,
                 vm((rows // 2, LANES), F32), square, square, square, square, vm((ROWS, LANES), F32),
-                vm((1, LANES), F32), vm((DEVICES, 1, LANES), F32),
-                dma((5,)), dma, dma((4,)), dma, dma((4,)), dma((3 + len(PIECES) - 1,)), dma, dma, pltpu.SemaphoreType.REGULAR,
+                vm((1, LANES), F32), vm((1, LANES), F32), vm((CHIPS, 1, LANES), F32), vm((2 * CHIPS - 1, 1, LANES), F32),
+                dma((5,)), dma, dma((4,)), dma, dma((4,)), dma((3 + len(PIECES) - 1,)), dma, dma, dma, pltpu.SemaphoreType.REGULAR,
             ],
             compiler_params=pltpu.CompilerParams(collective_id=0, has_side_effects=True, vmem_limit_bytes=40 * 2 ** 20),
         )(x, u, cz)

time: 28.5 us -> 28.4 us (level)
  no operation moved by 1% of the time
where the time goes in v6:
time: 28.4 us; the launch traced here: 28.3 us
  Pallas kernels  27.6 us (97%)
  between operations  0.64 us (2%)
    pallas_call x1, Pallas kernels, local_layer(): pl.pallas_call(kernel, out_shape=shapes, in_specs=[pl.BlockSpec(memory_sp...  26.6 us
    pallas_call x1, Pallas kernels, local_layer(): pl.pallas_call(writer, out_shape=shapes, in_specs=[any_spec] * 2, out_spe...  0.99 us

profile of v6, /device:TPU:1, one launch (start us, length us, event | category | flops | bytes accessed | tf_op | source)
XLA Modules:
  0.0 28.3 jit_solution(8965945563550398467)
XLA Ops:
  0.6 26.6 %shard_map.50 = (f32[2048,128]{1,0:T(8,128)S(1)}, f32[1,20]{1,0:T(1,128)S(1)}) custom-call(f32[2048,128]{1,0:T(8,128)} %bitcast.15, f32[8,20]{1,0:T(8,128)} %bitcast.16, s32[2,10]{1,0:T(2,128)} %bitcast.17), custom_call_target="tpu_custom_call" | custom-call | tf_op jit(solution)/shard_map/pallas_call | solution.py:531
  27.3 1.0 %shard_map.51 = (f32[2048,128]{1,0:T(8,128)}, f32[1,20]{1,0:T(1,128)}) custom-call(f32[2048,128]{1,0:T(8,128)S(1)} %get-tuple-element.6.state_ref, f32[1,20]{1,0:T(1,128)S(1)} %get-tuple-element.7.z_ref), custom_call_target="tpu_custom_call" | custom-call | tf_op jit(solution)/shard_map/pallas_call | solution.py:544

commit v7 on v6

--- a/solution.py
+++ b/solution.py
@@ -16,7 +16,6 @@
 CHUNKS = 4
 PIECES = (0, 16, 64, 112, 128)
 FIRST = CHUNK // 4
-EARLY = 0
 DEVICES = 8
 CHIPS = 4
 QUBITS = 20
@@ -75,8 +74,11 @@
 
 def kernel(x_hbm, u_hbm, cz_hbm, OUT, z_ref,
            BIG, u_ref, cz_ref, S, R2, T, SG, GM, KM, XC, ZC, TP, V, VP, VR, V7,
-           ld, sent_sem, s1r, cpr, fwr, s2r, zs, zr, zp, ready):
-    X, RB, XP, RP = [BIG.at[part] for part in range(4)]
+           ld, sent_sem, s1r, fwr, s2r, zs, zp, ready):
+    zr = ld.at[2]
+    piece_sems = [s1r.at[0], s1r.at[1], s1r.at[2], fwr.at[0]]
+    size = BIG.shape[0] // 4
+    X, RB, XP, RP = [BIG.at[pl.ds(part * size, size)] for part in range(4)]
     me = lax.axis_index('q')
     bit_y = me // 4
     bit_x = (me // 2) % 2
@@ -117,7 +119,7 @@
 
     def core_copy(half, k):
         rows = block_rows(half, sent(half, k))
-        return remote(X.at[rows], XP.at[rows], sent_sem, cpr, dev_c)
+        return remote(X.at[rows], XP.at[rows], sent_sem, fwr.at[0], dev_c)
 
     def forward(half, k):
         rows = block_rows(half, sent(half, k))
@@ -128,10 +130,10 @@
         if piece is None:
             return remote(S.at[half, chunk], R2.at[half, chunk], sent_sem, s2r.at[k], second_dev[half])
         rows = pl.ds(PIECES[piece], PIECES[piece + 1] - PIECES[piece])
-        return remote(S.at[half, chunk, :, rows], R2.at[half, chunk, :, rows], sent_sem, s2r.at[3 + piece], second_dev[half])
-
-    u_copy = pltpu.make_async_copy(u_hbm, u_ref, ld.at[3])
-    cz_copy = pltpu.make_async_copy(cz_hbm, cz_ref, ld.at[4])
+        return remote(S.at[half, chunk, :, rows], R2.at[half, chunk, :, rows], sent_sem, piece_sems[piece], second_dev[half])
+
+    u_copy = pltpu.make_async_copy(u_hbm, u_ref, zs)
+    cz_copy = pltpu.make_async_copy(cz_hbm, cz_ref, zp)
     last_chip = bit_y * bit_x
     beside = bit_y + bit_x - 2 * last_chip
     barrier = pltpu.get_barrier_semaphore()
@@ -297,10 +299,8 @@
         else:
             for half in range(2):
                 stage2(half, k - 1).start()
-        if k == 0:
-            wait_bytes(XP, cpr)
         with scope('w_fw'):
-            wait_bytes(RP.at[0:2 * CHUNK], fwr.at[k])
+            wait_bytes(BIG.at[0:2 * CHUNK + (0 if k else size)], fwr.at[k])
 
         for half in range(2):
             coefs = stage1_coefs[half]
@@ -410,9 +410,6 @@
     cross = (zero_pair, zero_pair)
     with scope('w_s2'):
         wait_bytes(R2.at[:, 0], s2r.at[0])
-    for piece in range(EARLY):
-        for half in range(2):
-            stage2(half, 3, piece).start()
     with scope('x0'):
         cross = lax.fori_loop(0, TILES, add_cross(0), cross, unroll=2)
     with scope('w_s2'):
@@ -471,12 +468,9 @@
     pl.when(bit_c == 1)(send_sum)
     pl.when(bit_c == 0)(lambda: z_part().start())
     pl.when(bit_c == 1)(spread_sum)
-    def send_pieces(low, high):
-        for piece in range(low, high):
-            for half in range(2):
-                stage2(half, 3, piece).start()
-
-    send_pieces(EARLY, len(PIECES) - 1)
+    for piece in range(len(PIECES) - 1):
+        for half in range(2):
+            stage2(half, 3, piece).start()
     with scope('own'):
         lax.fori_loop(0, TILES, step_own, 0)
         lax.fori_loop(0, TILES, step_mix, 0)
@@ -488,7 +482,7 @@
     for piece in range(len(PIECES) - 1):
         low, high = PIECES[piece], PIECES[piece + 1]
         with scope('w_s2'):
-            wait_bytes(R2.at[:, 0, :, low:high], s2r.at[3 + piece])
+            wait_bytes(R2.at[:, 0, :, low:high], piece_sems[piece])
         with scope('tail'):
             lax.fori_loop(low // SUB, high // SUB, add_received(3, tables[3], store_out), 0)
         if piece == len(PIECES) - 3:
@@ -534,10 +528,10 @@
             in_specs=[pl.BlockSpec(memory_space=pltpu.HBM)] * 3,
             out_specs=(pl.BlockSpec(memory_space=pltpu.VMEM), pl.BlockSpec(memory_space=pltpu.VMEM)),
             scratch_shapes=[
-                vm((4, rows, LANES), F32), pltpu.SMEM(u.shape, F32), pltpu.SMEM(cz.shape, jnp.int32), halves, halves, halves,
+                vm((4 * rows, LANES), F32), pltpu.SMEM(u.shape, F32), pltpu.SMEM(cz.shape, jnp.int32), halves, halves, halves,
                 vm((rows // 2, LANES), F32), square, square, square, square, vm((ROWS, LANES), F32),
                 vm((1, LANES), F32), vm((1, LANES), F32), vm((CHIPS, 1, LANES), F32), vm((2 * CHIPS - 1, 1, LANES), F32),
-                dma((5,)), dma, dma((4,)), dma, dma((4,)), dma((3 + len(PIECES) - 1,)), dma, dma, dma, pltpu.SemaphoreType.REGULAR,
+                dma((3,)), dma, dma((4,)), dma((4,)), dma((3,)), dma, dma, pltpu.SemaphoreType.REGULAR,
             ],
             compiler_params=pltpu.CompilerParams(collective_id=0, has_side_effects=True, vmem_limit_bytes=40 * 2 ** 20),
         )(x, u, cz)

time: 28.4 us -> 28.3 us (level)
  no operation moved by 1% of the time
where the time goes in v7:
time: 28.3 us; the launch traced here: 28.2 us
  Pallas kernels  27.6 us (98%)
  between operations  0.64 us (2%)
    pallas_call x1, Pallas kernels, local_layer(): pl.pallas_call(kernel, out_shape=shapes, in_specs=[pl.BlockSpec(memory_sp...  26.6 us
    pallas_call x1, Pallas kernels, local_layer(): pl.pallas_call(writer, out_shape=shapes, in_specs=[any_spec] * 2, out_spe...  0.99 us

profile of v7, /device:TPU:1, one launch (start us, length us, event | category | flops | bytes accessed | tf_op | source)
XLA Modules:
  0.0 28.2 jit_solution(17046606665557105545)
XLA Ops:
  0.6 26.6 %shard_map.50 = (f32[2048,128]{1,0:T(8,128)S(1)}, f32[1,20]{1,0:T(1,128)S(1)}) custom-call(f32[2048,128]{1,0:T(8,128)} %bitcast.15, f32[8,20]{1,0:T(8,128)} %bitcast.16, s32[2,10]{1,0:T(2,128)} %bitcast.17), custom_call_target="tpu_custom_call" | custom-call | tf_op jit(solution)/shard_map/pallas_call | solution.py:525
  27.2 1.0 %shard_map.51 = (f32[2048,128]{1,0:T(8,128)}, f32[1,20]{1,0:T(1,128)}) custom-call(f32[2048,128]{1,0:T(8,128)S(1)} %get-tuple-element.6.state_ref, f32[1,20]{1,0:T(1,128)S(1)} %get-tuple-element.7.z_ref), custom_call_target="tpu_custom_call" | custom-call | tf_op jit(solution)/shard_map/pallas_call | solution.py:538

commit v8 on v7

--- a/solution.py
+++ b/solution.py
@@ -18,6 +18,7 @@
 FIRST = CHUNK // 4
 DEVICES = 8
 CHIPS = 4
+OUT_PARTS = 32
 QUBITS = 20
 scope = jax.named_scope
 
@@ -74,9 +75,10 @@
 
 def kernel(x_hbm, u_hbm, cz_hbm, OUT, z_ref,
            BIG, u_ref, cz_ref, S, R2, T, SG, GM, KM, XC, ZC, TP, V, VP, VR, V7,
-           ld, sent_sem, s1r, fwr, s2r, zs, zp, ready):
+           ld, sent_sem, s1r, fw, s2r, zs, zp, ready):
     zr = ld.at[2]
-    piece_sems = [s1r.at[0], s1r.at[1], s1r.at[2], fwr.at[0]]
+    fwr = [fw, ld.at[0], ld.at[1], fw]
+    piece_sems = [s1r.at[0], s1r.at[1], s1r.at[2], ld.at[0]]
     size = BIG.shape[0] // 4
     X, RB, XP, RP = [BIG.at[pl.ds(part * size, size)] for part in range(4)]
     me = lax.axis_index('q')
@@ -119,11 +121,11 @@
 
     def core_copy(half, k):
         rows = block_rows(half, sent(half, k))
-        return remote(X.at[rows], XP.at[rows], sent_sem, fwr.at[0], dev_c)
+        return remote(X.at[rows], XP.at[rows], sent_sem, fw, dev_c)
 
     def forward(half, k):
         rows = block_rows(half, sent(half, k))
-        return remote(RB.at[rows], RP.at[rows], sent_sem, fwr.at[k], dev_c)
+        return remote(RB.at[rows], RP.at[rows], sent_sem, fwr[k], dev_c)
 
     def stage2(half, k, piece=None):
         chunk = sent(half, k)
@@ -134,6 +136,11 @@
 
     u_copy = pltpu.make_async_copy(u_hbm, u_ref, zs)
     cz_copy = pltpu.make_async_copy(cz_hbm, cz_ref, zp)
+    order = [(k, part) for k in range(CHUNKS) for part in range(1 if k else 2)]
+    for k, part in order:
+        for half in range(2):
+            load_copy(half, k, part).start()
+
     last_chip = bit_y * bit_x
     beside = bit_y + bit_x - 2 * last_chip
     barrier = pltpu.get_barrier_semaphore()
@@ -144,10 +151,6 @@
 
     signal(barrier, (dev_c,))
     pl.when(last_chip == 0)(lambda: signal(barrier, (dev_x, dev_y)))
-    order = [(k, part) for k in range(CHUNKS) for part in range(1 if k else 2)]
-    for k, part in order:
-        for half in range(2):
-            load_copy(half, k, part).start()
     u_copy.start()
     cz_copy.start()
 
@@ -300,7 +303,7 @@
             for half in range(2):
                 stage2(half, k - 1).start()
         with scope('w_fw'):
-            wait_bytes(BIG.at[0:2 * CHUNK + (0 if k else size)], fwr.at[k])
+            wait_bytes(BIG.at[0:2 * CHUNK + (0 if k else size)], fwr[k])
 
         for half in range(2):
             coefs = stage1_coefs[half]
@@ -501,11 +504,14 @@
 
 
 def writer(state_ref, z_ref, state_out, z_out, sems):
-    copies = [pltpu.make_async_copy(state_ref, state_out, sems.at[0]), pltpu.make_async_copy(z_ref, z_out, sems.at[1])]
-    for copy in copies:
-        copy.start()
-    for copy in copies:
-        copy.wait()
+    size = state_ref.shape[0] // OUT_PARTS
+    for part in range(OUT_PARTS):
+        rows = pl.ds(part * size, size)
+        pltpu.make_async_copy(state_ref.at[rows], state_out.at[rows], sems.at[0]).start(priority=part % 2)
+    copy = pltpu.make_async_copy(z_ref, z_out, sems.at[1])
+    copy.start()
+    pltpu.make_async_copy(state_ref, state_out, sems.at[0]).wait()
+    copy.wait()
 
 
 def solution(mesh):
@@ -531,7 +537,7 @@
                 vm((4 * rows, LANES), F32), pltpu.SMEM(u.shape, F32), pltpu.SMEM(cz.shape, jnp.int32), halves, halves, halves,
                 vm((rows // 2, LANES), F32), square, square, square, square, vm((ROWS, LANES), F32),
                 vm((1, LANES), F32), vm((1, LANES), F32), vm((CHIPS, 1, LANES), F32), vm((2 * CHIPS - 1, 1, LANES), F32),
-                dma((3,)), dma, dma((4,)), dma((4,)), dma((3,)), dma, dma, pltpu.SemaphoreType.REGULAR,
+                dma((3,)), dma, dma((4,)), dma, dma((3,)), dma, dma, pltpu.SemaphoreType.REGULAR,
             ],
             compiler_params=pltpu.CompilerParams(collective_id=0, has_side_effects=True, vmem_limit_bytes=40 * 2 ** 20),
         )(x, u, cz)

time: 28.3 us -> 28.2 us (level)
  no operation moved by 1% of the time
where the time goes in v8:
time: 28.2 us; the launch traced here: 28.1 us
  Pallas kernels  27.5 us (98%)
  between operations  0.64 us (2%)
    pallas_call x1, Pallas kernels, local_layer(): pl.pallas_call(kernel, out_shape=shapes, in_specs=[pl.BlockSpec(memory_sp...  26.5 us
    pallas_call x1, Pallas kernels, local_layer(): pl.pallas_call(writer, out_shape=shapes, in_specs=[any_spec] * 2, out_spe...  0.97 us

profile of v8, /device:TPU:1, one launch (start us, length us, event | category | flops | bytes accessed | tf_op | source)
XLA Modules:
  0.0 28.1 jit_solution(11793070116413827256)
XLA Ops:
  0.6 26.5 %shard_map.50 = (f32[2048,128]{1,0:T(8,128)S(1)}, f32[1,20]{1,0:T(1,128)S(1)}) custom-call(f32[2048,128]{1,0:T(8,128)} %bitcast.15, f32[8,20]{1,0:T(8,128)} %bitcast.16, s32[2,10]{1,0:T(2,128)} %bitcast.17), custom_call_target="tpu_custom_call" | custom-call | tf_op jit(solution)/shard_map/pallas_call | solution.py:531
  27.2 1.0 %shard_map.51 = (f32[2048,128]{1,0:T(8,128)}, f32[1,20]{1,0:T(1,128)}) custom-call(f32[2048,128]{1,0:T(8,128)S(1)} %get-tuple-element.6.state_ref, f32[1,20]{1,0:T(1,128)S(1)} %get-tuple-element.7.z_ref), custom_call_target="tpu_custom_call" | custom-call | tf_op jit(solution)/shard_map/pallas_call | solution.py:544

commit v9 on v8

--- a/solution.py
+++ b/solution.py
@@ -14,8 +14,8 @@
 ROWS = SUB * TILES
 CHUNK = 2 * ROWS
 CHUNKS = 4
-PIECES = (0, 16, 64, 112, 128)
-FIRST = CHUNK // 4
+PIECES = (0, 24, 96, 120, 128)
+FIRST = 3 * CHUNK // 16
 DEVICES = 8
 CHIPS = 4
 OUT_PARTS = 32
@@ -487,7 +487,7 @@
         with scope('w_s2'):
             wait_bytes(R2.at[:, 0, :, low:high], piece_sems[piece])
         with scope('tail'):
-            lax.fori_loop(low // SUB, high // SUB, add_received(3, tables[3], store_out), 0)
+            lax.fori_loop(low // SUB, high // SUB, add_received(3, tables[3], store_out), 0, unroll=2)
         if piece == len(PIECES) - 3:
             with scope('w_z'):
                 pl.when(bit_c == 0)(lambda: wait_bytes(VR, zr))

time: 28.2 us -> 28.2 us (level)
  no operation moved by 1% of the time
where the time goes in v9:
time: 28.2 us; the launch traced here: 28.1 us
  Pallas kernels  27.4 us (97%)
  between operations  0.64 us (2%)
    pallas_call x1, Pallas kernels, local_layer(): pl.pallas_call(kernel, out_shape=shapes, in_specs=[pl.BlockSpec(memory_sp...  26.5 us
    pallas_call x1, Pallas kernels, local_layer(): pl.pallas_call(writer, out_shape=shapes, in_specs=[any_spec] * 2, out_spe...  0.97 us

profile of v9, /device:TPU:1, one launch (start us, length us, event | category | flops | bytes accessed | tf_op | source)
XLA Modules:
  0.0 28.1 jit_solution(5617817999587668082)
XLA Ops:
  0.6 26.5 %shard_map.50 = (f32[2048,128]{1,0:T(8,128)S(1)}, f32[1,20]{1,0:T(1,128)S(1)}) custom-call(f32[2048,128]{1,0:T(8,128)} %bitcast.15, f32[8,20]{1,0:T(8,128)} %bitcast.16, s32[2,10]{1,0:T(2,128)} %bitcast.17), custom_call_target="tpu_custom_call" | custom-call | tf_op jit(solution)/shard_map/pallas_call | solution.py:531
  27.1 1.0 %shard_map.51 = (f32[2048,128]{1,0:T(8,128)}, f32[1,20]{1,0:T(1,128)}) custom-call(f32[2048,128]{1,0:T(8,128)S(1)} %get-tuple-element.6.state_ref, f32[1,20]{1,0:T(1,128)S(1)} %get-tuple-element.7.z_ref), custom_call_target="tpu_custom_call" | custom-call | tf_op jit(solution)/shard_map/pallas_call | solution.py:544

commit v10 on v9

--- a/solution.py
+++ b/solution.py
@@ -75,8 +75,8 @@
 
 def kernel(x_hbm, u_hbm, cz_hbm, OUT, z_ref,
            BIG, u_ref, cz_ref, S, R2, T, SG, GM, KM, XC, ZC, TP, V, VP, VR, V7,
-           ld, sent_sem, s1r, fw, s2r, zs, zp, ready):
-    zr = ld.at[2]
+           ld, sent_sem, s1r, fw, s2r, ready):
+    zr, zs, zp = ld.at[2], ld.at[1], s1r.at[3]
     fwr = [fw, ld.at[0], ld.at[1], fw]
     piece_sems = [s1r.at[0], s1r.at[1], s1r.at[2], ld.at[0]]
     size = BIG.shape[0] // 4
@@ -134,8 +134,8 @@
         rows = pl.ds(PIECES[piece], PIECES[piece + 1] - PIECES[piece])
         return remote(S.at[half, chunk, :, rows], R2.at[half, chunk, :, rows], sent_sem, piece_sems[piece], second_dev[half])
 
-    u_copy = pltpu.make_async_copy(u_hbm, u_ref, zs)
-    cz_copy = pltpu.make_async_copy(cz_hbm, cz_ref, zp)
+    u_copy = pltpu.make_async_copy(u_hbm, u_ref, s2r.at[0])
+    cz_copy = pltpu.make_async_copy(cz_hbm, cz_ref, s2r.at[1])
     order = [(k, part) for k in range(CHUNKS) for part in range(1 if k else 2)]
     for k, part in order:
         for half in range(2):
@@ -161,6 +161,9 @@
             if wait and (k, part) in waits:
                 index, size = waits[k, part]
                 wait_bytes(X.at[:size], ld.at[index])
+                if k:
+                    u_copy.wait()
+                    cz_copy.wait()
             if k == 0:
                 for half in halves:
                     stage1(half, k, part).start()
@@ -188,8 +191,6 @@
     for k in range(CHUNKS):
         for half in range(2):
             core_copy(half, k).start()
-    u_copy.wait()
-    cz_copy.wait()
 
     def entry(qubit, row, col):
         return u_ref[row * 2 + col, qubit], u_ref[4 + row * 2 + col, qubit]
@@ -537,7 +538,7 @@
                 vm((4 * rows, LANES), F32), pltpu.SMEM(u.shape, F32), pltpu.SMEM(cz.shape, jnp.int32), halves, halves, halves,
                 vm((rows // 2, LANES), F32), square, square, square, square, vm((ROWS, LANES), F32),
                 vm((1, LANES), F32), vm((1, LANES), F32), vm((CHIPS, 1, LANES), F32), vm((2 * CHIPS - 1, 1, LANES), F32),
-                dma((3,)), dma, dma((4,)), dma, dma((3,)), dma, dma, pltpu.SemaphoreType.REGULAR,
+                dma((3,)), dma, dma((4,)), dma, dma((3,)), pltpu.SemaphoreType.REGULAR,
             ],
             compiler_params=pltpu.CompilerParams(collective_id=0, has_side_effects=True, vmem_limit_bytes=40 * 2 ** 20),
         )(x, u, cz)

time: 28.2 us -> 28.2 us (level)
  no operation moved by 1% of the time
where the time goes in v10:
time: 28.2 us; the launch traced here: 28.1 us
  Pallas kernels  27.4 us (97%)
  between operations  0.64 us (2%)
    pallas_call x1, Pallas kernels, local_layer(): pl.pallas_call(kernel, out_shape=shapes, in_specs=[pl.BlockSpec(memory_sp...  26.5 us
    pallas_call x1, Pallas kernels, local_layer(): pl.pallas_call(writer, out_shape=shapes, in_specs=[any_spec] * 2, out_spe...  0.97 us

profile of v10, /device:TPU:1, one launch (start us, length us, event | category | flops | bytes accessed | tf_op | source)
XLA Modules:
  0.0 28.1 jit_solution(6993916622951472324)
XLA Ops:
  0.6 26.5 %shard_map.50 = (f32[2048,128]{1,0:T(8,128)S(1)}, f32[1,20]{1,0:T(1,128)S(1)}) custom-call(f32[2048,128]{1,0:T(8,128)} %bitcast.15, f32[8,20]{1,0:T(8,128)} %bitcast.16, s32[2,10]{1,0:T(2,128)} %bitcast.17), custom_call_target="tpu_custom_call" | custom-call | tf_op jit(solution)/shard_map/pallas_call | solution.py:532
  27.1 1.0 %shard_map.51 = (f32[2048,128]{1,0:T(8,128)}, f32[1,20]{1,0:T(1,128)}) custom-call(f32[2048,128]{1,0:T(8,128)S(1)} %get-tuple-element.6.state_ref, f32[1,20]{1,0:T(1,128)S(1)} %get-tuple-element.7.z_ref), custom_call_target="tpu_custom_call" | custom-call | tf_op jit(solution)/shard_map/pallas_call | solution.py:545

commit v11 on v10

--- a/solution.py
+++ b/solution.py
@@ -14,7 +14,7 @@
 ROWS = SUB * TILES
 CHUNK = 2 * ROWS
 CHUNKS = 4
-PIECES = (0, 24, 96, 120, 128)
+PIECES = (0, 56, 104, 120, 128)
 FIRST = 3 * CHUNK // 16
 DEVICES = 8
 CHIPS = 4
@@ -296,11 +296,11 @@
     for k in range(CHUNKS):
         with scope('w_s1'):
             wait_bytes(RB.at[0:2 * CHUNK], s1r.at[k])
-        for half in range(2):
-            forward(half, k).start()
         if k == 0:
             pl.when(bit_c == 1)(lambda: send_rest((0, 1)))
-        else:
+        for half in range(2):
+            forward(half, k).start()
+        if k:
             for half in range(2):
                 stage2(half, k - 1).start()
         with scope('w_fw'):

time: 28.2 us -> 28.2 us (level)
  no operation moved by 1% of the time
where the time goes in v11:
time: 28.2 us; the launch traced here: 28.1 us
  Pallas kernels  27.4 us (97%)
  between operations  0.64 us (2%)
    pallas_call x1, Pallas kernels, local_layer(): pl.pallas_call(kernel, out_shape=shapes, in_specs=[pl.BlockSpec(memory_sp...  26.5 us
    pallas_call x1, Pallas kernels, local_layer(): pl.pallas_call(writer, out_shape=shapes, in_specs=[any_spec] * 2, out_spe...  0.97 us

profile of v11, /device:TPU:1, one launch (start us, length us, event | category | flops | bytes accessed | tf_op | source)
XLA Modules:
  0.0 28.1 jit_solution(18328545526325603579)
XLA Ops:
  0.6 26.5 %shard_map.50 = (f32[2048,128]{1,0:T(8,128)S(1)}, f32[1,20]{1,0:T(1,128)S(1)}) custom-call(f32[2048,128]{1,0:T(8,128)} %bitcast.15, f32[8,20]{1,0:T(8,128)} %bitcast.16, s32[2,10]{1,0:T(2,128)} %bitcast.17), custom_call_target="tpu_custom_call" | custom-call | tf_op jit(solution)/shard_map/pallas_call | solution.py:532
  27.1 1.0 %shard_map.51 = (f32[2048,128]{1,0:T(8,128)}, f32[1,20]{1,0:T(1,128)}) custom-call(f32[2048,128]{1,0:T(8,128)S(1)} %get-tuple-element.6.state_ref, f32[1,20]{1,0:T(1,128)S(1)} %get-tuple-element.7.z_ref), custom_call_target="tpu_custom_call" | custom-call | tf_op jit(solution)/shard_map/pallas_call | solution.py:545
